TPU v7x, 32 devices: a whole 2x2x4 slice. The times are simulated.
32 devices in a mesh: dp: 16 (over z, x, core), tensor: 2 (over y).
Axes of the slice: x: 2, y: 2, z: 4, core: 2. Of those that a mesh axis runs over, the one named last changes fastest.
Arguments:
- hidden_in: bfloat16 [4096, 2048], P('dp'), may hold values from -6 to 6
- segments: int32 [16, 256], P('dp'), may hold values from 0 to 3, never falling along the last dimension, each value on 1 to 128 neighbouring positions
- expert_ids: int32 [4096, 6], P('dp'), may hold values from 0 to 15, all different within a row; in each aligned block of 256 rows (0 to 255, 256 to 511, ...) at most 144 rows name the same one
- grad_out: bfloat16 [4096, 2048], P('dp'), may hold values from -6 to 6
- attn_gain: bfloat16 [2048], P('dp'), may hold values from 0.5 to 1.5
- query_proj: bfloat16 [2048, 3072], P('dp', 'tensor'), may hold values from -0.125 to 0.125
- latent_down: bfloat16 [2048, 576], P('dp'), may hold values from -0.125 to 0.125
- latent_gain: bfloat16 [512], P('dp'), may hold values from 0.5 to 1.5
- latent_up: bfloat16 [512, 4096], P('dp', 'tensor'), may hold values from -0.25 to 0.25
- output_proj: bfloat16 [2048, 2048], P('tensor', 'dp'), may hold values from -0.375 to 0.375
- ffn_gain: bfloat16 [2048], P('dp'), may hold values from 0.5 to 1.5
- router_weight: bfloat16 [2048, 16], P('dp'), may hold values from -0.125 to 0.125
- shared_gate: bfloat16 [2048, 2816], P('dp', 'tensor'), may hold values from -0.125 to 0.125
- shared_up: bfloat16 [2048, 2816], P('dp', 'tensor'), may hold values from -0.125 to 0.125
- shared_down: bfloat16 [2816, 2048], P('tensor', 'dp'), may hold values from -0.109375 to 0.109375
- routed_gate_weight: bfloat16 [16, 2048, 1408], P('dp', None, 'tensor'), may hold values from -0.125 to 0.125
- routed_up_weight: bfloat16 [16, 2048, 1408], P('dp', None, 'tensor'), may hold values from -0.125 to 0.125
- routed_down_weight: bfloat16 [16, 1408, 2048], P('dp', 'tensor'), may hold values from -1 to 1
Outputs:
- output: bfloat16 [4096, 2048], P('dp')
- hidden_input_gradient: float32 [4096, 2048], P('dp')
- attention_gain_gradient: float32 [2048], P('dp')
- query_projection_gradient: float32 [2048, 3072], P('dp', 'tensor')
- latent_down_gradient: float32 [2048, 576], P('dp')
- grad_latent_gain: float32 [512], P('dp')
- grad_latent_up: float32 [512, 4096], P('dp', 'tensor')
- output_projection_gradient: float32 [2048, 2048], P('tensor', 'dp')
- feedforward_gain_gradient: float32 [2048], P('dp')
- router_weight_gradient: float32 [2048, 16], P('dp')
- grad_shared_gate: float32 [2048, 2816], P('dp', 'tensor')
- grad_shared_up: float32 [2048, 2816], P('dp', 'tensor')
- grad_shared_down: float32 [2816, 2048], P('tensor', 'dp')
- grad_expert_gate: float32 [16, 2048, 1408], P('dp', None, 'tensor')
- grad_expert_up: float32 [16, 2048, 1408], P('dp', None, 'tensor')
- grad_expert_down: float32 [16, 1408, 2048], P('dp', 'tensor')
Inputs may be any that keep to these rules, and one draw needn't show every extreme that they name: `expert_ids`: each row names 6 different experts. Within the rows of one device (aligned blocks of 256 rows) no expert is named by more than 144 rows, a bound that some block reaches. `segments`: segment numbers never fall along a sequence; a segment has 1 to 128 positions.
All inputs are finite; a program needn't handle non-finite values.
Results may differ from a plain program's by a relative error of at most 0.02.
Values may be sent and summed in bfloat16 or wider, within the bound.
A program may use at most 320 MiB of HBM per device.

v0:
```python
import jax
import jax.numpy as jnp
from jax import lax
from jax.sharding import PartitionSpec as P

NOPE = 128
ROPE = 64
DV = 128
LAT = 512


EPS = 1e-06
ROPE_BASE = 10000.0
NEG_FILL = -1e30


def rope_tables(length, width):
    half_width = width // 2
    frequency = ROPE_BASE ** (-(jnp.arange(half_width, dtype=jnp.float32) * (2.0 / width)))
    angles = jnp.arange(length, dtype=jnp.float32)[:, None] * frequency[None, :]
    angles = jnp.concatenate([angles, angles], axis=1)
    return (jnp.cos(angles), jnp.sin(angles))


def rotate(values, cos_table, sin_table):
    half_width = values.shape[-1] // 2
    turned = jnp.concatenate([-values[..., half_width:], values[..., :half_width]], axis=-1)
    return values * cos_table + turned * sin_table


def rms_recip(values):
    return lax.rsqrt(jnp.mean(values * values, axis=-1, keepdims=True) + EPS)


def rms_back(grad_normed, values, recip, gain):
    hat_values = values * recip
    scaled = grad_normed * gain
    grad_in = recip * (scaled - hat_values * jnp.mean(scaled * hat_values, axis=-1, keepdims=True))
    grad_gain = jnp.sum(grad_normed * hat_values, axis=0)
    return (grad_in, grad_gain)


def silu_parts(pre_act):
    sigmoid_val = jax.nn.sigmoid(pre_act)
    return (pre_act * sigmoid_val, sigmoid_val * (1.0 + pre_act * (1.0 - sigmoid_val)))


def slot_positions(chosen, experts):
    matches = (
        (chosen[:, :, None] == jnp.arange(experts, dtype=jnp.int32))
        .astype(jnp.int32)
        .reshape(-1, experts)
    )
    earlier = jnp.cumsum(matches, axis=0) - matches
    return jnp.sum(earlier * matches, axis=1).reshape(chosen.shape)


def mask_table(segments):
    places = jnp.arange(segments.shape[1], dtype=jnp.int32)
    same_doc = segments[:, :, None] == segments[:, None, :]
    return same_doc & (places[None, None, :] <= places[None, :, None])


def attend_scores(query_all, key_nope, key_rope, allowed):
    nope_width = key_nope.shape[-1]
    scale = query_all.shape[-1] ** (-0.5)
    scores = jnp.einsum(
        "sqhd,skhd->shqk", query_all[..., :nope_width], key_nope, preferred_element_type=jnp.float32
    )
    scores = scores + jnp.einsum(
        "sqhd,skd->shqk", query_all[..., nope_width:], key_rope, preferred_element_type=jnp.float32
    )
    return jnp.where(allowed[:, None], scores * scale, NEG_FILL)


def to_expert(arrived, sources, local_count):
    capacity = arrived.shape[1]
    feature_width = arrived.shape[2]
    grouped = arrived.reshape(sources, local_count, capacity, feature_width)
    return jnp.transpose(grouped, (1, 0, 2, 3)).reshape(
        local_count, sources * capacity, feature_width
    )


def from_expert(expert_rows, sources):
    local_count = expert_rows.shape[0]
    capacity = expert_rows.shape[1] // sources
    feature_width = expert_rows.shape[2]
    grouped = expert_rows.reshape(local_count, sources, capacity, feature_width)
    return jnp.transpose(grouped, (1, 0, 2, 3)).reshape(
        sources * local_count, capacity, feature_width
    )


def local(
    hidden_in,
    segments,
    expert_ids,
    grad_out,
    attn_gain,
    query_proj,
    latent_down,
    latent_gain,
    latent_up,
    output_proj,
    ffn_gain,
    router_weight,
    shared_gate,
    shared_up,
    shared_down,
    routed_gate_weight,
    routed_up_weight,
    routed_down_weight,
):
    float_type = jnp.float32
    low_type = jnp.bfloat16
    tok_count = hidden_in.shape[0]
    seq_count = segments.shape[0]
    seq_len = segments.shape[1]
    top_count = expert_ids.shape[1]
    head_dim = NOPE + ROPE
    dp_count = lax.axis_size("dp")
    local_experts = routed_gate_weight.shape[0]
    dense_weights = (
        attn_gain,
        query_proj,
        latent_down,
        latent_gain,
        latent_up,
        output_proj,
        ffn_gain,
        router_weight,
        shared_gate,
        shared_up,
        shared_down,
    )
    gathered = (
        lax.all_gather(dense_weights[0], "dp", axis=0, tiled=True),
        lax.all_gather(dense_weights[1], "dp", axis=0, tiled=True),
        lax.all_gather(dense_weights[2], "dp", axis=0, tiled=True),
        lax.all_gather(dense_weights[3], "dp", axis=0, tiled=True),
        lax.all_gather(dense_weights[4], "dp", axis=0, tiled=True),
        lax.all_gather(dense_weights[5], "dp", axis=1, tiled=True),
        lax.all_gather(dense_weights[6], "dp", axis=0, tiled=True),
        lax.all_gather(dense_weights[7], "dp", axis=0, tiled=True),
        lax.all_gather(dense_weights[8], "dp", axis=0, tiled=True),
        lax.all_gather(dense_weights[9], "dp", axis=0, tiled=True),
        lax.all_gather(dense_weights[10], "dp", axis=1, tiled=True),
    )
    (
        full_attn_gain,
        full_query,
        full_down,
        full_lgain,
        full_up,
        full_output,
        full_ffn_gain,
        full_router,
        full_sgate,
        full_sup,
        full_sdown,
    ) = gathered
    num_experts = full_router.shape[1]
    capacity = 3 * tok_count * top_count // (2 * num_experts)
    head_count = full_query.shape[1] // head_dim

    def by_seq(array):
        return array.reshape((seq_count, seq_len) + array.shape[1:])

    residual_in = hidden_in.astype(float_type)
    recip_one = rms_recip(residual_in)
    normed_one = (residual_in * recip_one * full_attn_gain.astype(float_type)).astype(low_type)
    cos_table, sin_table = rope_tables(seq_len, ROPE)
    cos_tok = jnp.tile(cos_table, (seq_count, 1))
    sin_tok = jnp.tile(sin_table, (seq_count, 1))
    query_raw = jnp.dot(normed_one, full_query, preferred_element_type=float_type).reshape(
        tok_count, head_count, head_dim
    )
    queries = jnp.concatenate(
        [query_raw[..., :NOPE], rotate(query_raw[..., NOPE:], cos_tok[:, None], sin_tok[:, None])],
        axis=-1,
    ).astype(low_type)
    down_raw = jnp.dot(normed_one, full_down, preferred_element_type=float_type)
    latent = down_raw[:, :LAT]
    recip_latent = rms_recip(latent)
    latent_normed = (latent * recip_latent * full_lgain.astype(float_type)).astype(low_type)
    key_rope = rotate(down_raw[:, LAT:], cos_tok, sin_tok).astype(low_type)
    keys_values = (
        jnp.dot(latent_normed, full_up, preferred_element_type=float_type)
        .astype(low_type)
        .reshape(tok_count, head_count, NOPE + DV)
    )
    key_nope = by_seq(keys_values[..., :NOPE])
    values = by_seq(keys_values[..., NOPE:])
    query_seq = by_seq(queries)
    rope_seq = by_seq(key_rope)
    allowed = mask_table(segments)
    scores = attend_scores(query_seq, key_nope, rope_seq, allowed)
    highest = jnp.max(scores, axis=-1, keepdims=True)
    log_total = highest + jnp.log(jnp.sum(jnp.exp(scores - highest), axis=-1, keepdims=True))
    attn_probs = jnp.exp(scores - log_total).astype(low_type)
    heads_out = jnp.einsum(
        "shqk,skhd->sqhd", attn_probs, values, preferred_element_type=float_type
    ).astype(low_type)
    attn_flat = heads_out.reshape(tok_count, head_count * DV)
    attn_part = jnp.dot(attn_flat, full_output, preferred_element_type=float_type)
    attn_full = lax.psum(attn_part, "tensor")
    mid = residual_in + attn_full
    recip_two = rms_recip(mid)
    normed_two = (mid * recip_two * full_ffn_gain.astype(float_type)).astype(low_type)
    logits = jnp.dot(normed_two, full_router, preferred_element_type=float_type)
    router_probs = jax.nn.softmax(logits, axis=-1)
    selector = (expert_ids[:, :, None] == jnp.arange(num_experts, dtype=jnp.int32)).astype(
        float_type
    )
    gate_weight = jnp.sum(selector * router_probs[:, None, :], axis=-1)
    shared_pre_gate = jnp.dot(normed_two, full_sgate, preferred_element_type=float_type)
    shared_pre_up = jnp.dot(normed_two, full_sup, preferred_element_type=float_type)
    shared_act, shared_slope = silu_parts(shared_pre_gate)
    shared_hidden = (shared_act * shared_pre_up).astype(low_type)
    shared_part = jnp.dot(shared_hidden, full_sdown, preferred_element_type=float_type)
    slots = slot_positions(expert_ids, num_experts)
    place_grid = expert_ids * capacity + slots
    places = place_grid.reshape(-1)
    place_rows = jnp.arange(num_experts * capacity, dtype=jnp.int32)
    dispatch_table = jnp.sum(
        (place_grid[None, :, :] == place_rows[:, None, None]).astype(low_type), axis=-1
    )
    send_rows = (
        jnp.dot(dispatch_table, normed_two, preferred_element_type=float_type)
        .astype(low_type)
        .reshape(num_experts, capacity, -1)
    )
    arrived = lax.all_to_all(send_rows, "dp", split_axis=0, concat_axis=0, tiled=True)
    expert_rows = to_expert(arrived, dp_count, local_experts)
    pre_gate = jnp.einsum(
        "erd,edf->erf", expert_rows, routed_gate_weight, preferred_element_type=float_type
    )
    pre_up = jnp.einsum(
        "erd,edf->erf", expert_rows, routed_up_weight, preferred_element_type=float_type
    )
    expert_act, expert_slope = silu_parts(pre_gate)
    expert_hidden = (expert_act * pre_up).astype(low_type)
    expert_result = jnp.einsum(
        "erf,efd->erd", expert_hidden, routed_down_weight, preferred_element_type=float_type
    ).astype(low_type)
    returned = lax.all_to_all(
        from_expert(expert_result, dp_count), "dp", split_axis=0, concat_axis=0, tiled=True
    )
    picked = (
        returned.reshape(num_experts * capacity, -1)[places]
        .reshape(tok_count, top_count, -1)
        .astype(float_type)
    )
    moe_part = jnp.sum(gate_weight[:, :, None] * picked, axis=1)
    ffn_full = lax.psum((moe_part + shared_part).astype(jnp.bfloat16), "tensor").astype(jnp.float32)
    output = (mid + ffn_full).astype(low_type)
    back_weights = (
        lax.all_gather(dense_weights[0], "dp", axis=0, tiled=True),
        lax.all_gather(dense_weights[1], "dp", axis=0, tiled=True),
        lax.all_gather(dense_weights[2], "dp", axis=0, tiled=True),
        lax.all_gather(dense_weights[3], "dp", axis=0, tiled=True),
        lax.all_gather(dense_weights[4], "dp", axis=0, tiled=True),
        lax.all_gather(dense_weights[5], "dp", axis=1, tiled=True),
        lax.all_gather(dense_weights[6], "dp", axis=0, tiled=True),
        lax.all_gather(dense_weights[7], "dp", axis=0, tiled=True),
        lax.all_gather(dense_weights[8], "dp", axis=0, tiled=True),
        lax.all_gather(dense_weights[9], "dp", axis=0, tiled=True),
        lax.all_gather(dense_weights[10], "dp", axis=1, tiled=True),
    )
    (
        back_attn_gain,
        back_query,
        back_down,
        back_lgain,
        back_up,
        back_output,
        back_ffn_gain,
        back_router,
        back_sgate,
        back_sup,
        back_sdown,
    ) = back_weights
    grad_float = grad_out.astype(float_type)
    shared_act_grad = jnp.dot(grad_out, back_sdown.T, preferred_element_type=float_type)
    shared_gate_grad = (shared_act_grad * shared_pre_up * shared_slope).astype(low_type)
    shared_up_grad = (shared_act_grad * shared_act).astype(low_type)
    shared_down_gradient = jnp.dot(shared_hidden.T, grad_out, preferred_element_type=float_type)
    shared_gate_gradient = jnp.dot(
        normed_two.T, shared_gate_grad, preferred_element_type=float_type
    )
    shared_up_gradient = jnp.dot(normed_two.T, shared_up_grad, preferred_element_type=float_type)
    shared_in_grad = jnp.dot(shared_gate_grad, back_sgate.T, preferred_element_type=float_type)
    shared_in_grad = shared_in_grad + jnp.dot(
        shared_up_grad, back_sup.T, preferred_element_type=float_type
    )
    weight_grad_part = jnp.sum(grad_float[:, None, :] * picked, axis=-1)
    slot_grad = (
        (gate_weight[:, :, None] * grad_float[:, None, :])
        .astype(low_type)
        .reshape(tok_count * top_count, -1)
    )
    grad_send = (
        jnp.zeros((num_experts * capacity, slot_grad.shape[1]), low_type)
        .at[places]
        .set(slot_grad)
        .reshape(num_experts, capacity, -1)
    )
    grad_arrived = to_expert(
        lax.all_to_all(grad_send, "dp", split_axis=0, concat_axis=0, tiled=True),
        dp_count,
        local_experts,
    )
    hidden_grad = jnp.einsum(
        "erd,efd->erf", grad_arrived, routed_down_weight, preferred_element_type=float_type
    )
    pre_gate_grad = (hidden_grad * pre_up * expert_slope).astype(low_type)
    pre_up_grad = (hidden_grad * expert_act).astype(low_type)
    routed_down_gradient = jnp.einsum(
        "erf,erd->efd", expert_hidden, grad_arrived, preferred_element_type=float_type
    )
    routed_gate_gradient = jnp.einsum(
        "erd,erf->edf", expert_rows, pre_gate_grad, preferred_element_type=float_type
    )
    routed_up_gradient = jnp.einsum(
        "erd,erf->edf", expert_rows, pre_up_grad, preferred_element_type=float_type
    )
    row_grad = jnp.einsum(
        "erf,edf->erd", pre_gate_grad, routed_gate_weight, preferred_element_type=float_type
    )
    row_grad = (
        row_grad
        + jnp.einsum(
            "erf,edf->erd", pre_up_grad, routed_up_weight, preferred_element_type=float_type
        )
    ).astype(low_type)
    grad_returned = lax.all_to_all(
        from_expert(row_grad, dp_count), "dp", split_axis=0, concat_axis=0, tiled=True
    )
    moe_in_grad = jnp.sum(
        grad_returned.reshape(num_experts * capacity, -1)[places]
        .reshape(tok_count, top_count, -1)
        .astype(float_type),
        axis=1,
    )
    normed_two_grad, weight_grad = lax.psum(
        (shared_in_grad + moe_in_grad, weight_grad_part), "tensor"
    )
    prob_grad = jnp.sum(selector * weight_grad[:, :, None], axis=1)
    logit_grad = (
        router_probs * (prob_grad - jnp.sum(prob_grad * router_probs, axis=-1, keepdims=True))
    ).astype(low_type)
    router_weight_gradient = jnp.dot(normed_two.T, logit_grad, preferred_element_type=float_type)
    normed_two_grad = normed_two_grad + jnp.dot(
        logit_grad, back_router.T, preferred_element_type=float_type
    )
    norm_two_back, feedforward_gain_gradient = rms_back(
        normed_two_grad, mid, recip_two, back_ffn_gain.astype(float_type)
    )
    mid_grad = grad_float + norm_two_back
    mid_low = mid_grad.astype(low_type)
    output_projection_gradient = jnp.dot(attn_flat.T, mid_low, preferred_element_type=float_type)
    heads_grad = by_seq(
        jnp.dot(mid_low, back_output.T, preferred_element_type=float_type)
        .astype(low_type)
        .reshape(tok_count, head_count, DV)
    )
    scale = head_dim ** (-0.5)
    scores = attend_scores(query_seq, key_nope, rope_seq, allowed)
    attn_probs = jnp.exp(scores - log_total)
    probs_low = attn_probs.astype(low_type)
    values_grad = jnp.einsum(
        "shqk,sqhd->skhd", probs_low, heads_grad, preferred_element_type=float_type
    )
    probs_grad = jnp.einsum(
        "sqhd,skhd->shqk", heads_grad, values, preferred_element_type=float_type
    )
    delta = jnp.sum(heads_grad.astype(float_type) * heads_out.astype(float_type), axis=-1)
    delta = jnp.transpose(delta, (0, 2, 1))[..., None]
    score_grad = (attn_probs * (probs_grad - delta) * scale).astype(low_type)
    nope_grad_q = jnp.einsum(
        "shqk,skhd->sqhd", score_grad, key_nope, preferred_element_type=float_type
    )
    rope_grad_q = jnp.einsum(
        "shqk,skd->sqhd", score_grad, rope_seq, preferred_element_type=float_type
    )
    key_nope_grad = jnp.einsum(
        "shqk,sqhd->skhd", score_grad, query_seq[..., :NOPE], preferred_element_type=float_type
    )
    key_rope_grad = jnp.einsum(
        "shqk,sqhd->skd", score_grad, query_seq[..., NOPE:], preferred_element_type=float_type
    )
    query_grad = jnp.concatenate([nope_grad_q, rope_grad_q], axis=-1).reshape(
        tok_count, head_count, head_dim
    )
    query_raw_grad = (
        jnp.concatenate(
            [
                query_grad[..., :NOPE],
                rotate(query_grad[..., NOPE:], cos_tok[:, None], -sin_tok[:, None]),
            ],
            axis=-1,
        )
        .astype(low_type)
        .reshape(tok_count, head_count * head_dim)
    )
    query_projection_gradient = jnp.dot(
        normed_one.T, query_raw_grad, preferred_element_type=float_type
    )
    kv_grad = (
        jnp.concatenate([key_nope_grad, values_grad], axis=-1)
        .astype(low_type)
        .reshape(tok_count, head_count * (NOPE + DV))
    )
    latent_up_gradient = jnp.dot(latent_normed.T, kv_grad, preferred_element_type=float_type)
    normed_one_part = jnp.dot(query_raw_grad, back_query.T, preferred_element_type=float_type)
    latent_part_grad = jnp.dot(kv_grad, back_up.T, preferred_element_type=float_type)
    rope_part_grad = key_rope_grad.reshape(tok_count, ROPE)
    normed_one_grad, latent_normed_grad, rope_key_grad = (
        lax.psum(normed_one_part.astype(jnp.bfloat16), "tensor").astype(jnp.float32),
        lax.psum(latent_part_grad.astype(jnp.bfloat16), "tensor").astype(jnp.float32),
        lax.psum(rope_part_grad.astype(jnp.bfloat16), "tensor").astype(jnp.float32),
    )
    latent_grad, latent_gain_gradient = rms_back(
        latent_normed_grad, latent, recip_latent, back_lgain.astype(float_type)
    )
    rope_pre_grad = rotate(rope_key_grad, cos_tok, -sin_tok)
    down_grad = jnp.concatenate([latent_grad, rope_pre_grad], axis=-1).astype(low_type)
    latent_down_gradient = jnp.dot(normed_one.T, down_grad, preferred_element_type=float_type)
    normed_one_grad = normed_one_grad + jnp.dot(
        down_grad, back_down.T, preferred_element_type=float_type
    )
    norm_one_back, attention_gain_gradient = rms_back(
        normed_one_grad, residual_in, recip_one, back_attn_gain.astype(float_type)
    )
    hidden_input_gradient = mid_grad + norm_one_back
    accumulated_total = tuple(
        (
            lax.psum_scatter(attention_gain_gradient, "dp", scatter_dimension=0, tiled=True),
            lax.psum_scatter(query_projection_gradient, "dp", scatter_dimension=0, tiled=True),
            lax.psum_scatter(latent_down_gradient, "dp", scatter_dimension=0, tiled=True),
            lax.psum_scatter(latent_gain_gradient, "dp", scatter_dimension=0, tiled=True),
            lax.psum_scatter(latent_up_gradient, "dp", scatter_dimension=0, tiled=True),
            lax.psum_scatter(output_projection_gradient, "dp", scatter_dimension=1, tiled=True),
            lax.psum_scatter(feedforward_gain_gradient, "dp", scatter_dimension=0, tiled=True),
            lax.psum_scatter(router_weight_gradient, "dp", scatter_dimension=0, tiled=True),
            lax.psum_scatter(shared_gate_gradient, "dp", scatter_dimension=0, tiled=True),
            lax.psum_scatter(shared_up_gradient, "dp", scatter_dimension=0, tiled=True),
            lax.psum_scatter(shared_down_gradient, "dp", scatter_dimension=1, tiled=True),
        )
    )
    return (
        (output, hidden_input_gradient)
        + accumulated_total
        + (routed_gate_gradient, routed_up_gradient, routed_down_gradient)
    )


def solution(mesh):
    return jax.shard_map(
        local,
        mesh=mesh,
        in_specs=(
            P("dp", None),
            P("dp", None),
            P("dp", None),
            P("dp", None),
            P("dp"),
            P("dp", "tensor"),
            P("dp", None),
            P("dp"),
            P("dp", "tensor"),
            P("tensor", "dp"),
            P("dp"),
            P("dp", None),
            P("dp", "tensor"),
            P("dp", "tensor"),
            P("tensor", "dp"),
            P("dp", None, "tensor"),
            P("dp", None, "tensor"),
            P("dp", "tensor", None),
        ),
        out_specs=(
            P("dp", None),
            P("dp", None),
            P("dp"),
            P("dp", "tensor"),
            P("dp", None),
            P("dp"),
            P("dp", "tensor"),
            P("tensor", "dp"),
            P("dp"),
            P("dp", None),
            P("dp", "tensor"),
            P("dp", "tensor"),
            P("tensor", "dp"),
            P("dp", None, "tensor"),
            P("dp", None, "tensor"),
            P("dp", "tensor", None),
        ),
        check_vma=False,
    )
```

profile of v0, /device:TPU:0, one launch (start us, length us, event | category | flops | bytes accessed | tf_op | source)
XLA Modules:
  0.0 2345.5 jit_solution(467236567790860397)
XLA Ops:
  10.1 23.3 all-gather
  36.3 30.3 %all-reduce = bf16[512]{0:T(512)(128)(2,1)S(1)} all-reduce(bf16[512]{0:T(512)(128)(2,1)S(1)} %dynamic-update-slice), channel_id=1, replica_groups=mesh['dp'=16,'tensor'=2] {'dp'}, use_global_device_ids=true, to_apply=%add | all-reduce | flops 512 | bytes 2048
  73.2 24.4 %all-gather.12.cloned.1.call-done = bf16[512,2048]{1,0:T(8,128)(2,1)} async-done(((bf16[32,2048]{1,0:T(8,128)(2,1)}), bf16[512,2048]{1,0:T(8,128)(2,1)}) %all-gather.12.cloned.1.call-update) | async-done | bytes 2097168 | tf_op jit(solution)/shard_map/all_gather | solution.py:142
  105.2 54.8 %all-gather.14.cloned.1.call-done = bf16[2048,1536]{1,0:T(8,128)(2,1)} async-done(((bf16[128,1536]{1,0:T(8,128)(2,1)}), bf16[2048,1536]{1,0:T(8,128)(2,1)}) %all-gather.14.cloned.1.call-update) | async-done | bytes 6291472 | tf_op jit(solution)/shard_map/all_gather | solution.py:139
  170.4 42.9 %all-gather.16.cloned.1.call-done = bf16[1024,2048]{1,0:T(8,128)(2,1)} async-done(((bf16[1024,128]{1,0:T(8,128)(2,1)}), bf16[1024,2048]{1,0:T(8,128)(2,1)}) %all-gather.16.cloned.1.call-update) | async-done | bytes 4194320 | tf_op jit(solution)/shard_map/all_gather | solution.py:143
  218.8 18.7 all-gather.1
  246.3 33.2 %all-reduce.10.cloned.1.call-done = f32[256,2048]{1,0:T(8,128)} async-done(((f32[256,2048]{1,0:T(8,128)}), f32[256,2048]{1,0:T(8,128)}) %all-reduce.10.cloned.1.call-update) | async-done | bytes 2097168 | tf_op jit(solution)/shard_map/psum | solution.py:207
  294.6 9.1 mul.399
  303.8 15.7 mul.400
  319.5 143.7 %all_gather.51 = bf16[2048,16]{0,1:T(8,128)(2,1)S(1)} all-gather(bf16[128,16]{0,1:T(8,128)(2,1)S(1)} %copy-done.74), channel_id=1, replica_groups=mesh['dp'=16,'tensor'=2] {'dp'}, dimensions={0}, use_global_device_ids=true | all-gather | bytes 69632 | tf_op jit(solution)/shard_map/all_gather | solution.py:145
  465.8 16.7 scatter_custom_fusion
  482.5 51.0 %all-to-all-start.2 = ((bf16[16,144,2048]{2,1,0:T(8,128)(2,1)}), bf16[16,144,2048]{2,1,0:T(8,128)(2,1)}, u32[]{:S(2)}, u32[]{:S(2)}) async-start(bf16[16,144,2048]{2,1,0:T(8,128)(2,1)} %bitcast.187), calls=%async_computation.2 | async-start | bytes 18874368 | tf_op jit(solution)/shard_map/all_to_all | solution.py:310
  533.5 13.1 fusion.14
  546.6 12.0 fusion.18
  558.6 143.7 %all-to-all-done.2 = bf16[16,144,2048]{2,1,0:T(8,128)(2,1)} async-done(((bf16[16,144,2048]{2,1,0:T(8,128)(2,1)}), bf16[16,144,2048]{2,1,0:T(8,128)(2,1)}, u32[]{:S(2)}, u32[]{:S(2)}) %all-to-all-start.2) | async-done | bytes 9437216 | tf_op jit(solution)/shard_map/all_to_all | solution.py:310
  702.3 16.4 multiply_convert_fusion.1
  718.8 10.8 fusion.16
  729.6 14.7 add_convert_fusion
  744.3 41.5 %all-to-all-start.3 = ((bf16[16,144,2048]{2,1,0:T(8,128)(2,1)}), bf16[16,144,2048]{2,1,0:T(8,128)(2,1)}, u32[]{:S(2)}, u32[]{:S(2)}) async-start(bf16[16,144,2048]{2,1,0:T(8,128)(2,1)} %bitcast.189), calls=%async_computation.3 | async-start | bytes 18874368 | tf_op jit(solution)/shard_map/all_to_all | solution.py:337
  787.2 11.9 convolution_convert_fusion
  799.1 202.0 %all-to-all-done.3 = bf16[16,144,2048]{2,1,0:T(8,128)(2,1)} async-done(((bf16[16,144,2048]{2,1,0:T(8,128)(2,1)}), bf16[16,144,2048]{2,1,0:T(8,128)(2,1)}, u32[]{:S(2)}, u32[]{:S(2)}) %all-to-all-start.3) | async-done | bytes 9437216 | tf_op jit(solution)/shard_map/all_to_all | solution.py:337
  1001.1 64.2 %all-to-all-start.1 = ((bf16[16,144,2048]{2,1,0:T(8,128)(2,1)}), bf16[16,144,2048]{2,1,0:T(8,128)(2,1)}, u32[]{:S(2)}, u32[]{:S(2)}) async-start(bf16[16,144,2048]{2,1,0:T(8,128)(2,1)} %bitcast.188), calls=%async_computation.1 | async-start | bytes 18874368 | tf_op jit(solution)/shard_map/all_to_all | solution.py:247
  1077.5 168.3 %all-gather.22.cloned.1.call-done = bf16[1408,2048]{1,0:T(8,128)(2,1)} async-done(((bf16[1408,128]{1,0:T(8,128)(2,1)}), bf16[1408,2048]{1,0:T(8,128)(2,1)}) %all-gather.22.cloned.1.call-update) | async-done | bytes 5767184 | tf_op jit(solution)/shard_map/all_gather | solution.py:148
  1255.6 18.0 gather_fusion.1
  1273.6 11.7 reshape.516
  1285.3 9.8 reduce_sum.194
  1295.1 7.0 fusion.20
  1303.8 17.6 gather_fusion
  1321.4 12.3 reshape.515
  1333.7 11.9 multiply_reduce_fusion
  1345.7 8.7 psum.52
  1354.6 7.1 fusion.21
  1361.7 18.1 all-reduce.12.cloned.1.call-done
  1395.9 7.2 psum.55
  1429.1 7.0 fusion.95
  1441.2 44.9 %all-reduce.14.cloned.1.call-done = (bf16[256,2048]{1,0:T(8,128)(2,1)}, bf16[256,2048]{1,0:T(8,128)(2,1)}, bf16[256,512]{0,1:T(8,128)(2,1)}) async-done(((bf16[256,2048]{1,0:T(8,128)(2,1)}, bf16[256,2048]{1,0:T(8,128)(2,1)}, bf16[256,512]{0,1:T(8,128)(2,1)}), (bf16[256,2048]{1,0:T(8,128)(2,1)}, bf16[256,2048]{1,0:T(8,128)(2,1)}, bf16[256,512]{0,1:T(8,128)(2,1)})) %all-reduce.14.cloned.1.call-update) | async-done | bytes 2359312 | tf_op jit(solution)/shard_map/psum | solution.py:256
  1499.3 8.0 fusion.78
  1508.6 13.2 convolution_bitcast_fusion.2
  1521.8 11.2 convolution_bitcast_fusion
  1533.0 11.2 convolution_bitcast_fusion.1
  1546.9 63.6 %all-reduce.4 = (f32[2048]{0:T(1024)S(1)}, f32[512]{0:T(512)S(1)}, f32[2048]{0:T(1024)S(1)}) all-reduce(f32[2048]{0:T(1024)S(1)} %get-tuple-element.20, f32[512]{0:T(512)S(1)} %get-tuple-element.22, f32[2048]{0:T(1024)S(1)} %get-tuple-element.18), channel_id=2, replica_groups=mesh['dp'=16,'tensor'=2] {'dp'}, use_global_device_ids=true, to_apply=%region_30.31.clone | all-reduce | flops 4608 | bytes 36864
  1619.8 131.1 %reduce-scatter.21.cloned.1.call-done = f32[128,1408]{1,0:T(8,128)} async-done(((f32[2048,1408]{1,0:T(8,128)}), f32[128,1408]{1,0:T(8,128)}) %reduce-scatter.21.cloned.1.call-update) | async-done | bytes 720912 | tf_op jit(solution)/shard_map/reduce_scatter | solution.py:448
  1750.8 130.9 %reduce-scatter.23.cloned.1.call-done = f32[1408,128]{1,0:T(8,128)} async-done(((f32[1408,2048]{1,0:T(8,128)}), f32[1408,128]{1,0:T(8,128)}) %reduce-scatter.23.cloned.1.call-update) | async-done | bytes 720912 | tf_op jit(solution)/shard_map/reduce_scatter | solution.py:449
  1881.8 55.0 %reduce-scatter.17.cloned.1.call-done = f32[128,16]{0,1:T(8,128)} async-done(((f32[2048,16]{0,1:T(8,128)}), f32[128,16]{0,1:T(8,128)}) %reduce-scatter.17.cloned.1.call-update) | async-done | bytes 8208 | tf_op jit(solution)/shard_map/reduce_scatter | solution.py:446
  1936.8 76.1 %reduce-scatter.13.cloned.1.call-done = f32[32,2048]{1,0:T(8,128)} async-done(((f32[512,2048]{1,0:T(8,128)}), f32[32,2048]{1,0:T(8,128)}) %reduce-scatter.13.cloned.1.call-update) | async-done | bytes 262160 | tf_op jit(solution)/shard_map/reduce_scatter | solution.py:443
  2012.9 79.0 %reduce-scatter.11.cloned.1.call-done = f32[128,576]{0,1:T(8,128)} async-done(((f32[2048,576]{0,1:T(8,128)}), f32[128,576]{0,1:T(8,128)}) %reduce-scatter.11.cloned.1.call-update) | async-done | bytes 294928 | tf_op jit(solution)/shard_map/reduce_scatter | solution.py:441
  2091.9 107.3 %reduce-scatter.15.cloned.1.call-done = f32[1024,128]{1,0:T(8,128)} async-done(((f32[1024,2048]{1,0:T(8,128)}), f32[1024,128]{1,0:T(8,128)}) %reduce-scatter.15.cloned.1.call-update) | async-done | bytes 524304 | tf_op jit(solution)/shard_map/reduce_scatter | solution.py:444
  2199.2 139.1 %reduce-scatter.9.cloned.1.call-done = f32[128,1536]{1,0:T(8,128)} async-done(((f32[2048,1536]{1,0:T(8,128)}), f32[128,1536]{1,0:T(8,128)}) %reduce-scatter.9.cloned.1.call-update) | async-done | bytes 786448 | tf_op jit(solution)/shard_map/reduce_scatter | solution.py:440
  (316 shorter events, 158.3 us)
Async XLA Ops:
  7.2 695.2 %copy-start = (bf16[1,704,2048]{2,1,0:T(8,128)(2,1)S(1)}, bf16[1,704,2048]{2,1,0:T(8,128)(2,1)}, u32[]{:S(2)}) copy-start(bf16[1,704,2048]{2,1,0:T(8,128)(2,1)} %param.35) | copy-start | bytes 8650756
  7.2 63.0 %all-gather.10.cloned.1.call-start = ((), (), s32[]{:S(2)}) async-start(), calls=%async_computation.12 | async-start | bytes 2506752 | tf_op jit(solution)/shard_map/all_gather | solution.py:140
  7.9 89.7 %all-gather.12.cloned.1.call-start = ((), (), s32[]{:S(2)}) async-start(), calls=%async_computation.13 | async-start | bytes 2228224 | tf_op jit(solution)/shard_map/all_gather | solution.py:142
  8.7 151.4 %all-gather.14.cloned.1.call-start = ((), (), s32[]{:S(2)}) async-start(), calls=%async_computation.14 | async-start | bytes 6684672 | tf_op jit(solution)/shard_map/all_gather | solution.py:139
  9.4 203.9 %all-gather.16.cloned.1.call-start = ((), (), s32[]{:S(2)}) async-start(), calls=%async_computation.15 | async-start | bytes 4456448 | tf_op jit(solution)/shard_map/all_gather | solution.py:143
  10.0 269.4 %all-reduce.10.cloned.1.call-start = ((), (), s32[]{:S(2)}) async-start(), calls=%async_computation.16 | async-start | bytes 4194304 | tf_op jit(solution)/shard_map/psum | solution.py:207
  33.4 126.7 %copy-start.49 = (f32[16,1,128]{2,1,0:T(1,128)}, f32[16,1,128]{2,1,0:T(1,128)S(1)}, u32[]{:S(2)}) copy-start(f32[16,1,128]{2,1,0:T(1,128)S(1)} %convert_element_type.241) | copy-start | bytes 24580
  66.5 31.1 %copy-start.64 = (f32[512]{0:T(512)}, f32[512]{0:T(512)S(1)}, u32[]{:S(2)}) copy-start(f32[512]{0:T(512)S(1)} %convert_element_type.192) | copy-start | bytes 6148
  68.1 92.0 %copy-start.62 = (f32[256]{0:T(256)}, f32[256]{0:T(256)S(1)}, u32[]{:S(2)}) copy-start(f32[256]{0:T(256)S(1)} %add_rsqrt_fusion.2) | copy-start | bytes 3076
  73.1 30.4 %copy-start.14 = (f32[256,576]{0,1:T(8,128)}, f32[256,576]{0,1:T(8,128)S(1)}, u32[]{:S(2)}) copy-start(f32[256,576]{0,1:T(8,128)S(1)} %fusion.82) | copy-start | bytes 1769476
  73.2 27.1 %copy-start.66 = (f32[256]{0:T(256)}, f32[256]{0:T(256)S(1)}, u32[]{:S(2)}) copy-start(f32[256]{0:T(256)S(1)} %add_rsqrt_fusion.1) | copy-start | bytes 3076
  105.2 60.8 %copy-start.45 = (f32[256,64]{0,1:T(8,128)}, f32[256,64]{0,1:T(8,128)S(1)}, u32[]{:S(2)}) copy-start(f32[256,64]{0,1:T(8,128)S(1)} %get-tuple-element.48) | copy-start | bytes 196612
  105.2 60.8 %copy-start.55 = (f32[256,64]{0,1:T(8,128)S(1)}, f32[256,64]{0,1:T(8,128)}, u32[]{:S(2)}) copy-start(f32[256,64]{0,1:T(8,128)} %get-tuple-element.50) | copy-start | bytes 196612
  170.4 47.7 %copy-start.20 = (bf16[8,128,256]{2,1,0:T(8,128)(2,1)}, bf16[8,128,256]{2,1,0:T(8,128)(2,1)S(1)}, u32[]{:S(2)}) copy-start(bf16[8,128,256]{2,1,0:T(8,128)(2,1)S(1)} %convolution_convert_fusion.6) | copy-start | bytes 1572868
  237.5 44.2 %copy-start.58 = (f32[16,1,128]{2,1,0:T(1,128)}, f32[16,1,128]{2,1,0:T(1,128)S(1)}, u32[]{:S(2)}) copy-start(f32[16,1,128]{2,1,0:T(1,128)S(1)} %convert_element_type.242) | copy-start | bytes 24580
  288.7 193.9 %all-to-all-start = ((bf16[16,144,2048]{2,1,0:T(8,128)(2,1)}), bf16[16,144,2048]{2,1,0:T(8,128)(2,1)}, u32[]{:S(2)}, u32[]{:S(2)}) async-start(bf16[16,144,2048]{2,1,0:T(8,128)(2,1)} %bitcast.186), calls=%async_computation | async-start | bytes 18874368 | tf_op jit(solution)/shard_map/all_to_all | solution.py:234
  464.9 17.7 copy-start.68
  482.5 219.8 %all-to-all-start.2 = ((bf16[16,144,2048]{2,1,0:T(8,128)(2,1)}), bf16[16,144,2048]{2,1,0:T(8,128)(2,1)}, u32[]{:S(2)}, u32[]{:S(2)}) async-start(bf16[16,144,2048]{2,1,0:T(8,128)(2,1)} %bitcast.187), calls=%async_computation.2 | async-start | bytes 18874368 | tf_op jit(solution)/shard_map/all_to_all | solution.py:310
  744.3 256.7 %all-to-all-start.3 = ((bf16[16,144,2048]{2,1,0:T(8,128)(2,1)}), bf16[16,144,2048]{2,1,0:T(8,128)(2,1)}, u32[]{:S(2)}, u32[]{:S(2)}) async-start(bf16[16,144,2048]{2,1,0:T(8,128)(2,1)} %bitcast.189), calls=%async_computation.3 | async-start | bytes 18874368 | tf_op jit(solution)/shard_map/all_to_all | solution.py:337
  785.9 280.5 %all-gather.18.cloned.1.call-start = ((), (), s32[]{:S(2)}) async-start(), calls=%async_computation.17 | async-start | bytes 6127616 | tf_op jit(solution)/shard_map/all_gather | solution.py:146
  786.4 285.5 %all-gather.20.cloned.1.call-start = ((), (), s32[]{:S(2)}) async-start(), calls=%async_computation.18 | async-start | bytes 6127616 | tf_op jit(solution)/shard_map/all_gather | solution.py:147
  1001.1 65.3 %copy-start.7 = (bf16[256,2048]{1,0:T(8,128)(2,1)S(1)}, bf16[256,2048]{1,0:T(8,128)(2,1)}, u32[]{:S(2)}) copy-start(bf16[256,2048]{1,0:T(8,128)(2,1)} %copy-done.6) | copy-start | bytes 3145732
  1001.1 302.7 %all-to-all-start.1 = ((bf16[16,144,2048]{2,1,0:T(8,128)(2,1)}), bf16[16,144,2048]{2,1,0:T(8,128)(2,1)}, u32[]{:S(2)}, u32[]{:S(2)}) async-start(bf16[16,144,2048]{2,1,0:T(8,128)(2,1)} %bitcast.188), calls=%async_computation.1 | async-start | bytes 18874368 | tf_op jit(solution)/shard_map/all_to_all | solution.py:247
  1065.3 180.5 %all-gather.22.cloned.1.call-start = ((), (), s32[]{:S(2)}) async-start(), calls=%async_computation.19 | async-start | bytes 6127616 | tf_op jit(solution)/shard_map/all_gather | solution.py:148
  1066.0 313.8 %all-reduce.12.cloned.1.call-start = ((), (), s32[]{:S(2)}) async-start(), calls=%async_computation.20 | async-start | bytes 4194304 | tf_op jit(solution)/shard_map/psum | solution.py:346
  1071.9 173.9 %copy-start.11 = (bf16[256,2048]{1,0:T(8,128)(2,1)S(1)}, bf16[256,2048]{1,0:T(8,128)(2,1)}, u32[]{:S(2)}) copy-start(bf16[256,2048]{1,0:T(8,128)(2,1)} %param.21) | copy-start | bytes 3145732
  1252.4 42.7 %copy-start.30 = (bf16[256,1408]{1,0:T(8,128)(2,1)}, bf16[256,1408]{1,0:T(8,128)(2,1)S(1)}, u32[]{:S(2)}) copy-start(bf16[256,1408]{1,0:T(8,128)(2,1)S(1)} %get-tuple-element.35) | copy-start | bytes 2162692
  1302.1 184.0 %all-reduce.14.cloned.1.call-start = ((), (), s32[]{:S(2)}) async-start(), calls=%async_computation.29 | async-start | bytes 4718592 | tf_op jit(solution)/shard_map/psum | solution.py:256
  1333.7 20.7 copy-start.61
  1333.7 20.8 copy-start.48
  1333.7 20.8 copy-start.69
  1333.7 20.8 copy-start.73
  1354.5 25.2 %copy-start.3 = (f32[256,2048]{1,0:T(8,128)S(1)}, f32[256,2048]{1,0:T(8,128)}, u32[]{:S(2)}) copy-start(f32[256,2048]{1,0:T(8,128)} %copy-done.2) | copy-start | bytes 6291460
  1354.6 25.2 %copy-start.44 = (bf16[2048,16]{0,1:T(8,128)(2,1)S(1)}, bf16[2048,16]{0,1:T(8,128)(2,1)}, u32[]{:S(2)}) copy-start(bf16[2048,16]{0,1:T(8,128)(2,1)} %copy-done.43) | copy-start | bytes 196612
  1354.6 25.2 %copy-start.59 = (f32[16,1,128]{2,1,0:T(1,128)S(1)}, f32[16,1,128]{2,1,0:T(1,128)}, u32[]{:S(2)}) copy-start(f32[16,1,128]{2,1,0:T(1,128)} %copy-done.58) | copy-start | bytes 24580
  1354.6 25.2 %copy-start.71 = (f32[256]{0:T(256)S(1)}, f32[256]{0:T(256)}, u32[]{:S(2)}) copy-start(f32[256]{0:T(256)} %copy-done.70) | copy-start | bytes 3076
  1413.3 206.5 %reduce-scatter.19.cloned.1.call-start = ((), (), s32[]{:S(2)}) async-start(), calls=%async_computation.26 | async-start | bytes 12255232 | tf_op jit(solution)/shard_map/reduce_scatter | solution.py:447
  1420.7 330.1 %reduce-scatter.21.cloned.1.call-start = ((), (), s32[]{:S(2)}) async-start(), calls=%async_computation.27 | async-start | bytes 12255232 | tf_op jit(solution)/shard_map/reduce_scatter | solution.py:448
  1427.9 453.9 %reduce-scatter.23.cloned.1.call-start = ((), (), s32[]{:S(2)}) async-start(), calls=%async_computation.28 | async-start | bytes 12255232 | tf_op jit(solution)/shard_map/reduce_scatter | solution.py:449
  1436.2 500.6 %reduce-scatter.17.cloned.1.call-start = ((), (), s32[]{:S(2)}) async-start(), calls=%async_computation.25 | async-start | bytes 139264 | tf_op jit(solution)/shard_map/reduce_scatter | solution.py:446
  1437.1 575.7 %reduce-scatter.13.cloned.1.call-start = ((), (), s32[]{:S(2)}) async-start(), calls=%async_computation.23 | async-start | bytes 4456448 | tf_op jit(solution)/shard_map/reduce_scatter | solution.py:443
  1441.2 47.4 %copy-start.9 = (bf16[256,2048]{1,0:T(8,128)(2,1)S(1)}, bf16[256,2048]{1,0:T(8,128)(2,1)}, u32[]{:S(2)}) copy-start(bf16[256,2048]{1,0:T(8,128)(2,1)} %param.18) | copy-start | bytes 3145732
  1441.2 47.4 %copy-start.50 = (f32[16,1,128]{2,1,0:T(1,128)S(1)}, f32[16,1,128]{2,1,0:T(1,128)}, u32[]{:S(2)}) copy-start(f32[16,1,128]{2,1,0:T(1,128)} %copy-done.49) | copy-start | bytes 24580
  1441.2 47.4 %copy-start.63 = (f32[256]{0:T(256)S(1)}, f32[256]{0:T(256)}, u32[]{:S(2)}) copy-start(f32[256]{0:T(256)} %copy-done.62) | copy-start | bytes 3076
  1441.2 650.7 %reduce-scatter.11.cloned.1.call-start = ((), (), s32[]{:S(2)}) async-start(), calls=%async_computation.22 | async-start | bytes 5013504 | tf_op jit(solution)/shard_map/reduce_scatter | solution.py:441
  1491.6 707.5 %reduce-scatter.15.cloned.1.call-start = ((), (), s32[]{:S(2)}) async-start(), calls=%async_computation.24 | async-start | bytes 8912896 | tf_op jit(solution)/shard_map/reduce_scatter | solution.py:444
  1498.1 840.2 %reduce-scatter.9.cloned.1.call-start = ((), (), s32[]{:S(2)}) async-start(), calls=%async_computation.21 | async-start | bytes 13369344 | tf_op jit(solution)/shard_map/reduce_scatter | solution.py:440
  1612.2 726.0 %copy-start.1 = (bf16[1,704,2048]{2,1,0:T(8,128)(2,1)S(1)}, bf16[1,704,2048]{2,1,0:T(8,128)(2,1)}, u32[]{:S(2)}) copy-start(bf16[1,704,2048]{2,1,0:T(8,128)(2,1)} %param.35) | copy-start | bytes 8650756
  (58 other events, 260.2 us)
Sparse Core Ops, SparseCore 0:
  10.2 45.0 all-gather.9
  57.4 40.1 all-gather.11
  99.9 60.1 all-gather.13
  162.1 51.1 all-gather.15
  218.2 61.1 all-reduce.9
  788.6 175.0 all-gather.17
  966.1 89.7 all-gather.19
  1068.3 177.4 all-gather.21
  1302.3 77.4 all-reduce.11
  1413.4 72.6 all-reduce.13
  1490.9 128.8 reduce-scatter.18
  1624.3 126.4 reduce-scatter.20
  1755.5 126.2 reduce-scatter.22
  1885.6 51.1 reduce-scatter.16
  1941.0 71.7 reduce-scatter.12
  2017.1 74.6 reduce-scatter.10
  2096.3 102.7 reduce-scatter.14
  2203.6 134.5 reduce-scatter.8
where the time goes:
time: 2360 us; the launch traced here: 2350 us
  waiting for transfers between devices  1460 us (62%)
  blocking collectives  295 us (12%)
  matrix products  233 us (10%)
  starting transfers between devices  164 us (7%)
  local copies, waits for them, and re-layouts  111 us (5%)
  other arithmetic  68 us (3%)
    all_to_all x1, waiting for transfers between devices, local(): lax.all_to_all(from_expert(row_grad, dp_count), 'dp', split_axis=0, conca...  202 us
    all_gather x1, waiting for transfers between devices, local(): lax.all_gather(dense_weights[10], 'dp', axis=1, tiled=True)  168 us
    all_to_all x1, waiting for transfers between devices, local(): lax.all_to_all(grad_send, 'dp', split_axis=0, concat_axis=0, tiled=True)  144 us
    all_gather x1, blocking collectives, local(): lax.all_gather(dense_weights[7], 'dp', axis=0, tiled=True)  144 us
    reduce_scatter x1, waiting for transfers between devices, local(): lax.psum_scatter(query_projection_gradient, 'dp', scatter_dimension=0, ti...  139 us
    reduce_scatter x1, waiting for transfers between devices, local(): lax.psum_scatter(shared_up_gradient, 'dp', scatter_dimension=0, tiled=True)  131 us
    reduce_scatter x1, waiting for transfers between devices, local(): lax.psum_scatter(shared_down_gradient, 'dp', scatter_dimension=1, tiled=T...  131 us
    reduce_scatter x1, waiting for transfers between devices, local(): lax.psum_scatter(output_projection_gradient, 'dp', scatter_dimension=1, t...  107 us
  transfers between devices with their start and end apart: 22, of which 17 were waited for; matrix products, arithmetic and copies ran while one was open for 14% of the time, Pallas kernels for 0%

commit v1 on v0

--- a/solution.py
+++ b/solution.py
@@ -45,6 +45,24 @@
     return (pre_act * sigmoid_val, sigmoid_val * (1.0 + pre_act * (1.0 - sigmoid_val)))
 
 
+def mask_table(segments):
+    places = jnp.arange(segments.shape[1], dtype=jnp.int32)
+    same_doc = segments[:, :, None] == segments[:, None, :]
+    return same_doc & (places[None, None, :] <= places[None, :, None])
+
+
+def attend_scores(query_all, key_nope, key_rope, allowed):
+    nope_width = key_nope.shape[-1]
+    scale = query_all.shape[-1] ** (-0.5)
+    scores = jnp.einsum(
+        "sqhd,skhd->shqk", query_all[..., :nope_width], key_nope, preferred_element_type=jnp.float32
+    )
+    scores = scores + jnp.einsum(
+        "sqhd,skd->shqk", query_all[..., nope_width:], key_rope, preferred_element_type=jnp.float32
+    )
+    return jnp.where(allowed[:, None], scores * scale, NEG_FILL)
+
+
 def slot_positions(chosen, experts):
     matches = (
         (chosen[:, :, None] == jnp.arange(experts, dtype=jnp.int32))
@@ -53,24 +71,6 @@
     )
     earlier = jnp.cumsum(matches, axis=0) - matches
     return jnp.sum(earlier * matches, axis=1).reshape(chosen.shape)
-
-
-def mask_table(segments):
-    places = jnp.arange(segments.shape[1], dtype=jnp.int32)
-    same_doc = segments[:, :, None] == segments[:, None, :]
-    return same_doc & (places[None, None, :] <= places[None, :, None])
-
-
-def attend_scores(query_all, key_nope, key_rope, allowed):
-    nope_width = key_nope.shape[-1]
-    scale = query_all.shape[-1] ** (-0.5)
-    scores = jnp.einsum(
-        "sqhd,skhd->shqk", query_all[..., :nope_width], key_nope, preferred_element_type=jnp.float32
-    )
-    scores = scores + jnp.einsum(
-        "sqhd,skd->shqk", query_all[..., nope_width:], key_rope, preferred_element_type=jnp.float32
-    )
-    return jnp.where(allowed[:, None], scores * scale, NEG_FILL)
 
 
 def to_expert(arrived, sources, local_count):
@@ -92,7 +92,7 @@
     )
 
 
-def local(
+def local_exchanged(
     hidden_in,
     segments,
     expert_ids,
@@ -456,6 +456,391 @@
     )
 
 
+def expert_tables(ids, expert, capacity):
+    match = jnp.any(ids == expert, axis=-1)
+    count = match.astype(jnp.int32)
+    place = jnp.where(match, jnp.cumsum(count, axis=-1) - count, capacity)
+    slots = jnp.arange(capacity, dtype=jnp.int32)
+    return (place[:, None, :] == slots[None, :, None]).astype(jnp.bfloat16)
+
+
+def gather_rows(table, tokens):
+    width = tokens.shape[1]
+    blocks = tokens.reshape(table.shape[0], table.shape[2], width)
+    rows = jnp.einsum("sct,std->scd", table, blocks, preferred_element_type=jnp.float32)
+    return rows.astype(jnp.bfloat16).reshape(-1, width)
+
+
+def place_rows(table, rows):
+    blocks = rows.reshape(table.shape[0], table.shape[1], -1)
+    spread = jnp.einsum("sct,scd->std", table, blocks, preferred_element_type=jnp.float32)
+    return spread.reshape(-1, spread.shape[-1])
+
+
+def local_gathered(
+    hidden_in,
+    segments,
+    expert_ids,
+    grad_out,
+    attn_gain,
+    query_proj,
+    latent_down,
+    latent_gain,
+    latent_up,
+    output_proj,
+    ffn_gain,
+    router_weight,
+    shared_gate,
+    shared_up,
+    shared_down,
+    routed_gate_weight,
+    routed_up_weight,
+    routed_down_weight,
+):
+    float_type = jnp.float32
+    low_type = jnp.bfloat16
+    tok_count = hidden_in.shape[0]
+    width = hidden_in.shape[1]
+    seq_count = segments.shape[0]
+    seq_len = segments.shape[1]
+    top_count = expert_ids.shape[1]
+    head_dim = NOPE + ROPE
+    dp_count = lax.axis_size("dp")
+    my_dp = lax.axis_index("dp")
+    local_experts = routed_gate_weight.shape[0]
+    num_experts = router_weight.shape[1]
+    capacity = 3 * tok_count * top_count // (2 * num_experts)
+    d_part = query_proj.shape[0]
+    lat_part = latent_up.shape[0]
+    hid_slice = shared_gate.shape[1] // dp_count
+
+    small = jnp.concatenate(
+        [
+            attn_gain,
+            ffn_gain,
+            latent_gain,
+            router_weight.reshape(-1),
+            expert_ids.T.reshape(-1).astype(low_type),
+        ]
+    )
+    small_all = lax.all_gather(small, "dp", axis=0, tiled=False)
+    cuts = [d_part, d_part, lat_part, d_part * num_experts, tok_count * top_count]
+    pieces, at = [], 0
+    for size in cuts:
+        pieces.append(small_all[:, at : at + size])
+        at += size
+    full_attn_gain = pieces[0].reshape(-1).astype(float_type)
+    full_ffn_gain = pieces[1].reshape(-1).astype(float_type)
+    full_lgain = pieces[2].reshape(-1).astype(float_type)
+    full_router = pieces[3].reshape(width, num_experts)
+    ids_all = jnp.transpose(
+        pieces[4].reshape(dp_count, top_count, tok_count).astype(jnp.int32), (0, 2, 1)
+    )
+    full_query = lax.all_gather(query_proj, "dp", axis=0, tiled=True)
+    full_down = lax.all_gather(latent_down, "dp", axis=0, tiled=True)
+    full_up = lax.all_gather(latent_up, "dp", axis=0, tiled=True)
+    full_output_t = lax.all_gather(output_proj.T, "dp", axis=0, tiled=True)
+
+    shared_send = jnp.concatenate(
+        [
+            shared_gate.reshape(d_part, dp_count, hid_slice),
+            shared_up.reshape(d_part, dp_count, hid_slice),
+            shared_down.T.reshape(d_part, dp_count, hid_slice),
+        ],
+        axis=-1,
+    )
+    shared_mine = lax.all_to_all(
+        jnp.transpose(shared_send, (1, 0, 2)), "dp", split_axis=0, concat_axis=0, tiled=True
+    ).reshape(width, 3 * hid_slice)
+    gate_up_w = shared_mine[:, : 2 * hid_slice]
+    down_w_t = shared_mine[:, 2 * hid_slice :]
+    grad_all = lax.all_gather(grad_out, "dp", axis=0, tiled=True)
+
+    def by_seq(array):
+        return array.reshape((seq_count, seq_len) + array.shape[1:])
+
+    residual_in = hidden_in.astype(float_type)
+    recip_one = rms_recip(residual_in)
+    normed_one = (residual_in * recip_one * full_attn_gain).astype(low_type)
+    cos_table, sin_table = rope_tables(seq_len, ROPE)
+    cos_tok = jnp.tile(cos_table, (seq_count, 1))
+    sin_tok = jnp.tile(sin_table, (seq_count, 1))
+    head_count = full_query.shape[1] // head_dim
+    query_raw = jnp.dot(normed_one, full_query, preferred_element_type=float_type).reshape(
+        tok_count, head_count, head_dim
+    )
+    queries = jnp.concatenate(
+        [query_raw[..., :NOPE], rotate(query_raw[..., NOPE:], cos_tok[:, None], sin_tok[:, None])],
+        axis=-1,
+    ).astype(low_type)
+    down_raw = jnp.dot(normed_one, full_down, preferred_element_type=float_type)
+    latent = down_raw[:, :LAT]
+    recip_latent = rms_recip(latent)
+    latent_normed = (latent * recip_latent * full_lgain).astype(low_type)
+    key_rope = rotate(down_raw[:, LAT:], cos_tok, sin_tok).astype(low_type)
+    keys_values = (
+        jnp.dot(latent_normed, full_up, preferred_element_type=float_type)
+        .astype(low_type)
+        .reshape(tok_count, head_count, NOPE + DV)
+    )
+    key_nope = by_seq(keys_values[..., :NOPE])
+    values = by_seq(keys_values[..., NOPE:])
+    query_seq = by_seq(queries)
+    rope_seq = by_seq(key_rope)
+    allowed = mask_table(segments)
+    scores = attend_scores(query_seq, key_nope, rope_seq, allowed)
+    highest = jnp.max(scores, axis=-1, keepdims=True)
+    log_total = highest + jnp.log(jnp.sum(jnp.exp(scores - highest), axis=-1, keepdims=True))
+    attn_probs = jnp.exp(scores - log_total)
+    probs_low = attn_probs.astype(low_type)
+    heads_out = jnp.einsum(
+        "shqk,skhd->sqhd", probs_low, values, preferred_element_type=float_type
+    ).astype(low_type)
+    attn_flat = heads_out.reshape(tok_count, head_count * DV)
+    attn_part = lax.dot_general(
+        attn_flat, full_output_t, (((1,), (1,)), ((), ())), preferred_element_type=float_type
+    )
+    attn_full = lax.psum(attn_part.astype(low_type), "tensor").astype(float_type)
+    mid = residual_in + attn_full
+    recip_two = rms_recip(mid)
+    normed_two = (mid * recip_two * full_ffn_gain).astype(low_type)
+    tok_all = lax.all_gather(normed_two, "dp", axis=0, tiled=True)
+
+    logits_all = jnp.dot(tok_all, full_router, preferred_element_type=float_type)
+    probs_all = jax.nn.softmax(logits_all, axis=-1)
+    router_probs = jax.nn.softmax(
+        jnp.dot(normed_two, full_router, preferred_element_type=float_type), axis=-1
+    )
+
+    pre_all = jnp.dot(tok_all, gate_up_w, preferred_element_type=float_type)
+    shared_pre_up = pre_all[:, hid_slice:]
+    shared_act, shared_slope = silu_parts(pre_all[:, :hid_slice])
+    shared_hidden = (shared_act * shared_pre_up).astype(low_type)
+    shared_act_grad = jnp.dot(grad_all, down_w_t, preferred_element_type=float_type)
+    shared_grads = jnp.concatenate(
+        [shared_act_grad * shared_pre_up * shared_slope, shared_act_grad * shared_act], axis=-1
+    ).astype(low_type)
+    ffn_part = lax.dot_general(
+        shared_hidden, down_w_t, (((1,), (1,)), ((), ())), preferred_element_type=float_type
+    )
+    in_grad_part = lax.dot_general(
+        shared_grads, gate_up_w, (((1,), (1,)), ((), ())), preferred_element_type=float_type
+    )
+
+    expert_columns, routed_grads = [], []
+    for index in range(local_experts):
+        expert = my_dp * local_experts + index
+        gate_w = routed_gate_weight[index]
+        up_w = routed_up_weight[index]
+        down_w = routed_down_weight[index]
+        table = expert_tables(ids_all, expert, capacity)
+        token_rows = gather_rows(table, tok_all)
+        grad_rows = gather_rows(table, grad_all).astype(float_type)
+        column = jnp.sum(
+            jnp.where(jnp.arange(num_experts, dtype=jnp.int32) == expert, probs_all, 0.0), axis=-1
+        ).reshape(dp_count, 1, tok_count)
+        gate_of = jnp.sum(table.astype(float_type) * column, axis=-1).reshape(-1, 1)
+        pre_gate = jnp.dot(token_rows, gate_w, preferred_element_type=float_type)
+        pre_up = jnp.dot(token_rows, up_w, preferred_element_type=float_type)
+        expert_act, expert_slope = silu_parts(pre_gate)
+        expert_hidden = (expert_act * pre_up).astype(low_type)
+        expert_result = jnp.dot(expert_hidden, down_w, preferred_element_type=float_type).astype(
+            low_type
+        )
+        result_float = expert_result.astype(float_type)
+        weight_rows = jnp.sum(grad_rows * result_float, axis=-1).reshape(dp_count, capacity, 1)
+        expert_columns.append(jnp.sum(table.astype(float_type) * weight_rows, axis=1))
+        ffn_part = ffn_part + place_rows(table, (gate_of * result_float).astype(low_type))
+        slot_grad = (gate_of * grad_rows).astype(low_type)
+        hidden_grad = lax.dot_general(
+            slot_grad, down_w, (((1,), (1,)), ((), ())), preferred_element_type=float_type
+        )
+        pre_gate_grad = (hidden_grad * pre_up * expert_slope).astype(low_type)
+        pre_up_grad = (hidden_grad * expert_act).astype(low_type)
+        row_grad = lax.dot_general(
+            pre_gate_grad, gate_w, (((1,), (1,)), ((), ())), preferred_element_type=float_type
+        )
+        row_grad = row_grad + lax.dot_general(
+            pre_up_grad, up_w, (((1,), (1,)), ((), ())), preferred_element_type=float_type
+        )
+        in_grad_part = in_grad_part + place_rows(table, row_grad.astype(low_type))
+        routed_grads.append(
+            (
+                jnp.dot(token_rows.T, pre_gate_grad, preferred_element_type=float_type),
+                jnp.dot(token_rows.T, pre_up_grad, preferred_element_type=float_type),
+                jnp.dot(expert_hidden.T, slot_grad, preferred_element_type=float_type),
+            )
+        )
+    routed_out = tuple(jnp.stack(parts) for parts in zip(*routed_grads))
+
+    prob_send = jnp.stack(expert_columns, axis=1)
+    prob_part = jnp.transpose(
+        lax.all_to_all(prob_send, "dp", split_axis=0, concat_axis=0, tiled=True).reshape(
+            num_experts, tok_count
+        )
+    )
+    prob_grad = lax.psum(prob_part, "tensor")
+    in_grad = lax.psum_scatter(
+        in_grad_part.astype(low_type), "dp", scatter_dimension=0, tiled=True
+    )
+    normed_two_grad = lax.psum(in_grad, "tensor").astype(float_type)
+    ffn_sum = lax.psum_scatter(ffn_part.astype(low_type), "dp", scatter_dimension=0, tiled=True)
+    ffn_full = lax.psum(ffn_sum, "tensor").astype(float_type)
+    output = (mid + ffn_full).astype(low_type)
+
+    shared_gate_up_grad = jnp.dot(tok_all.T, shared_grads, preferred_element_type=float_type)
+    shared_down_grad_t = jnp.dot(grad_all.T, shared_hidden, preferred_element_type=float_type)
+    shared_back = jnp.concatenate([shared_gate_up_grad, shared_down_grad_t], axis=-1).astype(
+        low_type
+    )
+    shared_back = lax.all_to_all(
+        shared_back.reshape(dp_count, d_part, 3 * hid_slice),
+        "dp",
+        split_axis=0,
+        concat_axis=0,
+        tiled=True,
+    )
+    shared_back = jnp.transpose(shared_back, (1, 0, 2)).astype(float_type)
+    shared_gate_gradient = shared_back[..., :hid_slice].reshape(d_part, -1)
+    shared_up_gradient = shared_back[..., hid_slice : 2 * hid_slice].reshape(d_part, -1)
+    shared_down_gradient = shared_back[..., 2 * hid_slice :].reshape(d_part, -1).T
+
+    grad_float = grad_out.astype(float_type)
+    logit_grad = (
+        router_probs * (prob_grad - jnp.sum(prob_grad * router_probs, axis=-1, keepdims=True))
+    ).astype(low_type)
+    router_weight_gradient = jnp.dot(normed_two.T, logit_grad, preferred_element_type=float_type)
+    normed_two_grad = normed_two_grad + jnp.dot(
+        logit_grad, full_router.T, preferred_element_type=float_type
+    )
+    norm_two_back, feedforward_gain_gradient = rms_back(
+        normed_two_grad, mid, recip_two, full_ffn_gain
+    )
+    mid_grad = grad_float + norm_two_back
+    mid_low = mid_grad.astype(low_type)
+    output_projection_gradient_t = jnp.dot(
+        mid_low.T, attn_flat, preferred_element_type=float_type
+    )
+    heads_grad = by_seq(
+        jnp.dot(mid_low, full_output_t, preferred_element_type=float_type)
+        .astype(low_type)
+        .reshape(tok_count, head_count, DV)
+    )
+    scale = head_dim ** (-0.5)
+    values_grad = jnp.einsum(
+        "shqk,sqhd->skhd", probs_low, heads_grad, preferred_element_type=float_type
+    )
+    probs_grad = jnp.einsum(
+        "sqhd,skhd->shqk", heads_grad, values, preferred_element_type=float_type
+    )
+    delta = jnp.sum(heads_grad.astype(float_type) * heads_out.astype(float_type), axis=-1)
+    delta = jnp.transpose(delta, (0, 2, 1))[..., None]
+    score_grad = (attn_probs * (probs_grad - delta) * scale).astype(low_type)
+    nope_grad_q = jnp.einsum(
+        "shqk,skhd->sqhd", score_grad, key_nope, preferred_element_type=float_type
+    )
+    rope_grad_q = jnp.einsum(
+        "shqk,skd->sqhd", score_grad, rope_seq, preferred_element_type=float_type
+    )
+    key_nope_grad = jnp.einsum(
+        "shqk,sqhd->skhd", score_grad, query_seq[..., :NOPE], preferred_element_type=float_type
+    )
+    key_rope_grad = jnp.einsum(
+        "shqk,sqhd->skd", score_grad, query_seq[..., NOPE:], preferred_element_type=float_type
+    )
+    query_grad = jnp.concatenate([nope_grad_q, rope_grad_q], axis=-1).reshape(
+        tok_count, head_count, head_dim
+    )
+    query_raw_grad = (
+        jnp.concatenate(
+            [
+                query_grad[..., :NOPE],
+                rotate(query_grad[..., NOPE:], cos_tok[:, None], -sin_tok[:, None]),
+            ],
+            axis=-1,
+        )
+        .astype(low_type)
+        .reshape(tok_count, head_count * head_dim)
+    )
+    query_projection_gradient = jnp.dot(
+        normed_one.T, query_raw_grad, preferred_element_type=float_type
+    )
+    kv_grad = (
+        jnp.concatenate([key_nope_grad, values_grad], axis=-1)
+        .astype(low_type)
+        .reshape(tok_count, head_count * (NOPE + DV))
+    )
+    latent_up_gradient = jnp.dot(latent_normed.T, kv_grad, preferred_element_type=float_type)
+    normed_one_part = lax.dot_general(
+        query_raw_grad, full_query, (((1,), (1,)), ((), ())), preferred_element_type=float_type
+    )
+    latent_part_grad = lax.dot_general(
+        kv_grad, full_up, (((1,), (1,)), ((), ())), preferred_element_type=float_type
+    )
+    rope_part_grad = key_rope_grad.reshape(tok_count, ROPE)
+    parts = jnp.concatenate(
+        [normed_one_part, latent_part_grad, rope_part_grad], axis=-1
+    ).astype(low_type)
+    sums = lax.psum(parts, "tensor").astype(float_type)
+    normed_one_grad = sums[:, :width]
+    latent_normed_grad = sums[:, width : width + LAT]
+    rope_key_grad = sums[:, width + LAT :]
+    latent_grad, latent_gain_gradient = rms_back(
+        latent_normed_grad, latent, recip_latent, full_lgain
+    )
+    rope_pre_grad = rotate(rope_key_grad, cos_tok, -sin_tok)
+    down_grad = jnp.concatenate([latent_grad, rope_pre_grad], axis=-1).astype(low_type)
+    latent_down_gradient = jnp.dot(normed_one.T, down_grad, preferred_element_type=float_type)
+    normed_one_grad = normed_one_grad + lax.dot_general(
+        down_grad, full_down, (((1,), (1,)), ((), ())), preferred_element_type=float_type
+    )
+    norm_one_back, attention_gain_gradient = rms_back(
+        normed_one_grad, residual_in, recip_one, full_attn_gain
+    )
+    hidden_input_gradient = mid_grad + norm_one_back
+
+    def scatter(array):
+        return lax.psum_scatter(
+            array.astype(low_type), "dp", scatter_dimension=0, tiled=True
+        ).astype(float_type)
+
+    small_grads = jnp.concatenate(
+        [
+            attention_gain_gradient.reshape(dp_count, -1),
+            feedforward_gain_gradient.reshape(dp_count, -1),
+            latent_gain_gradient.reshape(dp_count, -1),
+            router_weight_gradient.reshape(dp_count, -1),
+        ],
+        axis=-1,
+    )
+    small_sums = lax.psum_scatter(small_grads, "dp", scatter_dimension=0, tiled=True).reshape(-1)
+    one, two, three = d_part, 2 * d_part, 2 * d_part + lat_part
+    return (
+        output,
+        hidden_input_gradient,
+        small_sums[:one],
+        scatter(query_projection_gradient),
+        scatter(latent_down_gradient),
+        small_sums[two:three],
+        scatter(latent_up_gradient),
+        scatter(output_projection_gradient_t).T,
+        small_sums[one:two],
+        small_sums[three:].reshape(d_part, num_experts),
+        shared_gate_gradient,
+        shared_up_gradient,
+        shared_down_gradient,
+    ) + routed_out
+
+
+def local(*arrays):
+    tok_count, top_count = arrays[0].shape[0], arrays[2].shape[1]
+    gathered_rows = lax.axis_size("dp") * tok_count
+    slot_rows = 3 * tok_count * top_count // 2
+    if gathered_rows <= 2 * slot_rows:
+        return local_gathered(*arrays)
+    return local_exchanged(*arrays)
+
+
 def solution(mesh):
     return jax.shard_map(
         local,

time: 2360 us -> 1750 us (0.74)
  blocking collectives: 295 us -> 8.92 us
  waiting for transfers between devices: 1460 us -> 1180 us
  starting transfers between devices: 164 us -> 16.5 us
  matrix products: 233 us -> 313 us
  local copies, waits for them, and re-layouts: 111 us -> 150 us
    all_to_all x4 -> x3, waiting for transfers between devices: 346 us -> 45.5 us  [the longest x1 39.1 us: local_gathered(): lax.all_to_all(jnp.transpose(shared_send, (1, 0, 2)), 'dp', split_axis=0,...]
    reduce_scatter x8 -> x5, waiting for transfers between devices: 720 us -> 481 us  [the longest x3 220 us: scatter(): lax.psum_scatter(array.astype(low_type), 'dp', scatter_dimension=0, tiled...]
    all_gather x3 -> x0, blocking collectives: 186 us -> none  [the longest x1 144 us: local(): lax.all_gather(dense_weights[7], 'dp', axis=0, tiled=True)]
    all_to_all x4 -> x3, starting transfers between devices: 162 us -> 15.4 us  [the longest x1 5.87 us: local_gathered(): lax.all_to_all(shared_back.reshape(dp_count, d_part, 3 * hid_slice), 'dp'...]
    unnamed x18 -> x20, waiting for transfers between devices: 4.67 us -> 151 us
    all_gather x7 -> x6, waiting for transfers between devices: 290 us -> 393 us  [the longest x1 118 us: local_gathered(): tok_all = lax.all_gather(normed_two, 'dp', axis=0, tiled=True)]
    unnamed x2 -> x0, blocking collectives: 93.9 us -> none
    reshape x3 -> x9, local copies, waits for them, and re-layouts: 0.36 us -> 90.9 us  [the longest x2 63.4 us: place_rows(): return spread.reshape(-1, spread.shape[-1])]
  transfers between devices with their start and end apart: 22 -> 20, of which waited for: 17 -> 18; matrix products, arithmetic and copies ran while one was open for 14% -> 15% of each run, Pallas kernels for 0% -> 0%
where the time goes in v1:
time: 1750 us; the launch traced here: 1740 us
  waiting for transfers between devices  1180 us (67%)
  matrix products  313 us (18%)
  local copies, waits for them, and re-layouts  150 us (9%)
  other arithmetic  57.4 us (3%)
    reduce_scatter x3, waiting for transfers between devices, scatter(): lax.psum_scatter(array.astype(low_type), 'dp', scatter_dimension=0, tiled...  220 us
    reduce_scatter x1, waiting for transfers between devices, local_gathered(): lax.psum_scatter(ffn_part.astype(low_type), 'dp', scatter_dimension=0, ti...  154 us
    unnamed x20, waiting for transfers between devices  151 us
    all_gather x1, waiting for transfers between devices, local_gathered(): tok_all = lax.all_gather(normed_two, 'dp', axis=0, tiled=True)  118 us
    reduce_scatter x1, waiting for transfers between devices, local_gathered(): lax.psum_scatter(in_grad_part.astype(low_type), 'dp', scatter_dimension=0...  107 us
    all_gather x1, waiting for transfers between devices, local_gathered(): grad_all = lax.all_gather(grad_out, 'dp', axis=0, tiled=True)  93.2 us
    psum x1, waiting for transfers between devices, local_gathered(): ffn_full = lax.psum(ffn_sum, 'tensor').astype(float_type)  68 us
    reshape x2, local copies, waits for them, and re-layouts, place_rows(): return spread.reshape(-1, spread.shape[-1])  63.4 us
  transfers between devices with their start and end apart: 20, of which 18 were waited for; matrix products, arithmetic and copies ran while one was open for 15% of the time, Pallas kernels for 0%

profile of v1, /device:TPU:0, one launch (start us, length us, event | category | flops | bytes accessed | tf_op | source)
XLA Modules:
  0.0 1739.4 jit_solution(1068484538185161699)
XLA Ops:
  22.1 82.5 %all-reduce.13.cloned.1.call-done = bf16[61952]{0:T(1024)(128)(2,1)} async-done(((bf16[61952]{0:T(1024)(128)(2,1)}), bf16[61952]{0:T(1024)(128)(2,1)}) %all-reduce.13.cloned.1.call-update) | async-done | bytes 123920
  105.8 45.2 %all-gather.8.cloned.1.call-done = bf16[2048,576]{0,1:T(8,128)(2,1)} async-done(((bf16[128,576]{0,1:T(8,128)(2,1)}), bf16[2048,576]{0,1:T(8,128)(2,1)}) %all-gather.8.cloned.1.call-update) | async-done | bytes 2359312 | tf_op jit(solution)/shard_map/all_gather | solution.py:540
  154.0 39.6 %all-gather.10.cloned.1.call-done = bf16[512,2048]{1,0:T(8,128)(2,1)} async-done(((bf16[32,2048]{1,0:T(8,128)(2,1)}), bf16[512,2048]{1,0:T(8,128)(2,1)}) %all-gather.10.cloned.1.call-update) | async-done | bytes 2097168 | tf_op jit(solution)/shard_map/all_gather | solution.py:541
  201.2 54.7 %all-gather.12.cloned.1.call-done = bf16[2048,1536]{1,0:T(8,128)(2,1)} async-done(((bf16[128,1536]{1,0:T(8,128)(2,1)}), bf16[2048,1536]{1,0:T(8,128)(2,1)}) %all-gather.12.cloned.1.call-update) | async-done | bytes 6291472 | tf_op jit(solution)/shard_map/all_gather | solution.py:539
  255.8 6.1 fusion.85
  266.5 42.6 %all-gather.14.cloned.1.call-done = bf16[2048,1024]{0,1:T(8,128)(2,1)} async-done(((bf16[128,1024]{0,1:T(8,128)(2,1)}), bf16[2048,1024]{0,1:T(8,128)(2,1)}) %all-gather.14.cloned.1.call-update) | async-done | bytes 4194320 | tf_op jit(solution)/shard_map/all_gather | solution.py:542
  314.8 37.6 %all-reduce.9.cloned.1.call-done = bf16[256,2048]{0,1:T(8,128)(2,1)} async-done(((bf16[256,2048]{0,1:T(8,128)(2,1)}), bf16[256,2048]{0,1:T(8,128)(2,1)}) %all-reduce.9.cloned.1.call-update) | async-done | bytes 1048592 | tf_op jit(solution)/shard_map/psum | solution.py:603
  361.8 5.7 all-to-all-start
  369.5 39.1 %all-to-all-done = bf16[16,128,264]{1,2,0:T(8,128)(2,1)} async-done(((bf16[16,128,264]{1,2,0:T(8,128)(2,1)}), bf16[16,128,264]{1,2,0:T(8,128)(2,1)}, u32[]{:S(2)}, u32[]{:S(2)}) %all-to-all-start) | async-done | bytes 1081376 | tf_op jit(solution)/shard_map/all_to_all | solution.py:552
  410.9 93.2 %all-gather.18.cloned.1.call-done = bf16[4096,2048]{1,0:T(8,128)(2,1)} async-done(((bf16[256,2048]{1,0:T(8,128)(2,1)}), bf16[4096,2048]{1,0:T(8,128)(2,1)}) %all-gather.18.cloned.1.call-update) | async-done | bytes 16777232 | tf_op jit(solution)/shard_map/all_gather | solution.py:557
  504.1 12.0 convolution_convert_fusion.2
  516.1 118.2 %all-gather.16.cloned.1.call-done = bf16[4096,2048]{0,1:T(8,128)(2,1)} async-done(((bf16[256,2048]{0,1:T(8,128)(2,1)}), bf16[4096,2048]{0,1:T(8,128)(2,1)}) %all-gather.16.cloned.1.call-update) | async-done | bytes 16777232 | tf_op jit(solution)/shard_map/all_gather | solution.py:607
  634.4 8.1 fusion.93
  642.7 22.6 %copy.223 = bf16[4096,2048]{1,0:T(8,128)(2,1)} copy(bf16[4096,2048]{0,1:T(8,128)(2,1)} %all-gather.16.cloned.1.call-done) | data formatting | bytes 33554432 | tf_op jit(solution)/shard_map/reshape | solution.py:469
  665.3 12.0 convolution_convert_fusion.3
  677.3 10.3 fusion.17
  687.7 16.2 multiply_convert_fusion.2
  703.9 12.7 fusion.1
  718.2 8.8 fusion.2
  727.0 14.7 multiply_convert_fusion
  741.8 10.7 fusion.15
  752.5 14.3 add_convert_fusion.2
  766.8 16.9 fusion.21
  783.7 31.6 %copy.225 = f32[4096,2048]{0,1:T(8,128)} copy(f32[4096,2048]{1,0:T(8,128)} %bitcast.237) | data formatting | bytes 67108864 | tf_op jit(solution)/shard_map/reshape | solution.py:477
  815.3 10.5 fusion.50
  825.8 12.8 multiply_convert_fusion.5
  838.6 17.6 %add_convert_fusion = bf16[4096,2048]{0,1:T(8,128)(2,1)} fusion(f32[4096,2048]{0,1:T(8,128)} %copy.225, bf16[4096,88]{0,1:T(8,128)(2,1)} %get-tuple-element.93, bf16[4096,88]{0,1:T(8,128)(2,1)S(1)} %get-tuple-element.92, bf16[2048,264]{0,1:T(8,128)(2,1)S(1)} %copy-done.13), kind=kOutput, calls=%fused_computation | convolution fusion | flops 2972450816 | bytes 52494336 | tf_op jit(solution)/shard_map/dot_general | solution.py:626
  856.3 17.4 fusion.3
  873.7 19.2 %fusion.22 = f32[16,256,2048]{2,1,0:T(8,128)} fusion(bf16[16,144,2048]{2,1,0:T(8,128)(2,1)} %bitcast.242, s32[16,256]{1,0:T(8,128)S(1)} %fusion.73), kind=kOutput, calls=%fused_computation.56 | convolution fusion | flops 2416508928 | bytes 43008000 | tf_op jit(solution)/shard_map/sct,scd->std/dot_general | solution.py:476
  893.0 31.8 %copy.224 = f32[4096,2048]{0,1:T(8,128)} copy(f32[4096,2048]{1,0:T(8,128)} %bitcast.236) | data formatting | bytes 67108864 | tf_op jit(solution)/shard_map/reshape | solution.py:477
  924.7 106.9 %reduce-scatter.11.cloned.1.call-done = bf16[256,2048]{0,1:T(8,128)(2,1)} async-done(((bf16[4096,2048]{0,1:T(8,128)(2,1)}), bf16[256,2048]{0,1:T(8,128)(2,1)}) %reduce-scatter.11.cloned.1.call-update) | async-done | bytes 1048592 | tf_op jit(solution)/shard_map/reduce_scatter | solution.py:683
  1031.8 16.9 add_convert_fusion.1
  1057.3 6.4 all-to-all-done.1
  1063.8 8.9 psum.38
  1093.7 5.7 convolution_convert_fusion.8
  1100.5 154.2 %reduce-scatter.9.cloned.1.call-done = bf16[256,2048]{0,1:T(8,128)(2,1)} async-done(((bf16[4096,2048]{0,1:T(8,128)(2,1)}), bf16[256,2048]{0,1:T(8,128)(2,1)}) %reduce-scatter.9.cloned.1.call-update) | async-done | bytes 1048592 | tf_op jit(solution)/shard_map/reduce_scatter | solution.py:687
  1258.1 68.0 %all-reduce.17.cloned.1.call-done = (bf16[256,2048]{0,1:T(8,128)(2,1)}, bf16[256,2624]{0,1:T(8,128)(2,1)}) async-done(((bf16[256,2048]{0,1:T(8,128)(2,1)}, bf16[256,2624]{0,1:T(8,128)(2,1)}), (bf16[256,2048]{0,1:T(8,128)(2,1)}, bf16[256,2624]{0,1:T(8,128)(2,1)})) %all-reduce.17.cloned.1.call-update) | async-done | bytes 2392080 | tf_op jit(solution)/shard_map/psum | solution.py:688
  1331.2 5.3 fusion.29
  1359.2 8.7 fusion.42
  1368.0 11.5 fusion.39
  1380.8 5.9 all-to-all-start.2
  1386.7 12.1 convolution_bitcast_fusion.1
  1398.8 11.2 convolution_bitcast_fusion.2
  1410.0 8.6 convolution_bitcast_fusion.3
  1439.7 60.4 %reduce-scatter.15.cloned.1.call-done = bf16[32,2048]{1,0:T(8,128)(2,1)} async-done(((bf16[512,2048]{1,0:T(8,128)(2,1)}), bf16[32,2048]{1,0:T(8,128)(2,1)}) %reduce-scatter.15.cloned.1.call-update) | async-done | bytes 131088 | tf_op jit(solution)/shard_map/reduce_scatter | solution.py:803
  1501.8 65.2 %reduce-scatter.19.cloned.1.call-done = bf16[128,576]{1,0:T(8,128)(2,1)} async-done(((bf16[2048,576]{1,0:T(8,128)(2,1)}), bf16[128,576]{1,0:T(8,128)(2,1)}) %reduce-scatter.19.cloned.1.call-update) | async-done | bytes 147472
  1568.7 73.7 %reduce-scatter.17.cloned.1.call-done = bf16[128,1024]{1,0:T(8,128)(2,1)} async-done(((bf16[2048,1024]{1,0:T(8,128)(2,1)}), bf16[128,1024]{1,0:T(8,128)(2,1)}) %reduce-scatter.17.cloned.1.call-update) | async-done | bytes 262160 | tf_op jit(solution)/shard_map/reduce_scatter | solution.py:803
  1644.5 86.0 %reduce-scatter.13.cloned.1.call-done = bf16[128,1536]{1,0:T(8,128)(2,1)} async-done(((bf16[2048,1536]{1,0:T(8,128)(2,1)}), bf16[128,1536]{1,0:T(8,128)(2,1)}) %reduce-scatter.13.cloned.1.call-update) | async-done | bytes 393232 | tf_op jit(solution)/shard_map/reduce_scatter | solution.py:803
  (328 shorter events, 142.6 us)
Async XLA Ops:
  7.2 696.7 %copy-start = (bf16[1,704,2048]{2,1,0:T(8,128)(2,1)S(1)}, bf16[1,704,2048]{2,1,0:T(8,128)(2,1)}, u32[]{:S(2)}) copy-start(bf16[1,704,2048]{2,1,0:T(8,128)(2,1)} %param.35) | copy-start | bytes 8650756
  7.2 97.4 %all-reduce.13.cloned.1.call-start = ((), (), s32[]{:S(2)}) async-start(), calls=%async_computation.22 | async-start | bytes 249856
  14.1 136.9 %all-gather.8.cloned.1.call-start = ((), (), s32[]{:S(2)}) async-start(), calls=%async_computation.9 | async-start | bytes 2506752 | tf_op jit(solution)/shard_map/all_gather | solution.py:540
  14.9 178.7 %all-gather.10.cloned.1.call-start = ((), (), s32[]{:S(2)}) async-start(), calls=%async_computation.10 | async-start | bytes 2228224 | tf_op jit(solution)/shard_map/all_gather | solution.py:541
  15.6 240.3 %all-gather.12.cloned.1.call-start = ((), (), s32[]{:S(2)}) async-start(), calls=%async_computation.11 | async-start | bytes 6684672 | tf_op jit(solution)/shard_map/all_gather | solution.py:539
  16.2 292.9 %all-gather.14.cloned.1.call-start = ((), (), s32[]{:S(2)}) async-start(), calls=%async_computation.12 | async-start | bytes 4456448 | tf_op jit(solution)/shard_map/all_gather | solution.py:542
  16.8 335.7 %all-reduce.9.cloned.1.call-start = ((), (), s32[]{:S(2)}) async-start(), calls=%async_computation.13 | async-start | bytes 2097152 | tf_op jit(solution)/shard_map/psum | solution.py:603
  20.6 133.2 %copy-start.61 = (f32[256]{0:T(256)}, f32[256]{0:T(256)S(1)}, u32[]{:S(2)}) copy-start(f32[256]{0:T(256)S(1)} %add_rsqrt_fusion.2) | copy-start | bytes 3076
  105.7 45.3 %copy-start.41 = (bf16[16,3872]{1,0:T(8,128)(2,1)}, bf16[16,3872]{1,0:T(8,128)(2,1)S(1)}, u32[]{:S(2)}) copy-start(bf16[16,3872]{1,0:T(8,128)(2,1)S(1)} %reshape.521) | copy-start | bytes 371716
  105.8 87.7 %copy-start.56 = (f32[512]{0:T(512)}, f32[512]{0:T(512)S(1)}, u32[]{:S(2)}) copy-start(f32[512]{0:T(512)S(1)} %reshape.516) | copy-start | bytes 6148
  105.8 150.0 %copy-start.50 = (f32[2048]{0:T(1024)}, f32[2048]{0:T(1024)S(1)}, u32[]{:S(2)}) copy-start(f32[2048]{0:T(1024)S(1)} %get-tuple-element.111) | copy-start | bytes 24580
  105.8 248.7 %copy-start.54 = (f32[2048]{0:T(1024)}, f32[2048]{0:T(1024)S(1)}, u32[]{:S(2)}) copy-start(f32[2048]{0:T(1024)S(1)} %get-tuple-element.110) | copy-start | bytes 24580
  153.9 45.6 %copy-start.11 = (f32[256,576]{0,1:T(8,128)}, f32[256,576]{0,1:T(8,128)S(1)}, u32[]{:S(2)}) copy-start(f32[256,576]{0,1:T(8,128)S(1)} %fusion.87) | copy-start | bytes 1769476
  154.0 42.3 %copy-start.59 = (f32[256]{0:T(256)}, f32[256]{0:T(256)S(1)}, u32[]{:S(2)}) copy-start(f32[256]{0:T(256)S(1)} %add_rsqrt_fusion.1) | copy-start | bytes 3076
  201.2 60.9 %copy-start.39 = (f32[256,64]{0,1:T(8,128)}, f32[256,64]{0,1:T(8,128)S(1)}, u32[]{:S(2)}) copy-start(f32[256,64]{0,1:T(8,128)S(1)} %get-tuple-element.115) | copy-start | bytes 196612
  201.2 60.9 %copy-start.49 = (f32[256,64]{0,1:T(8,128)S(1)}, f32[256,64]{0,1:T(8,128)}, u32[]{:S(2)}) copy-start(f32[256,64]{0,1:T(8,128)} %get-tuple-element.114) | copy-start | bytes 196612
  266.5 47.5 %copy-start.17 = (bf16[8,128,256]{2,1,0:T(8,128)(2,1)}, bf16[8,128,256]{2,1,0:T(8,128)(2,1)S(1)}, u32[]{:S(2)}) copy-start(bf16[8,128,256]{2,1,0:T(8,128)(2,1)S(1)} %convolution_convert_fusion.14) | copy-start | bytes 1572868
  314.0 190.1 %all-gather.18.cloned.1.call-start = ((), (), s32[]{:S(2)}) async-start(), calls=%async_computation.16 | async-start | bytes 17825792 | tf_op jit(solution)/shard_map/all_gather | solution.py:557
  314.8 319.6 %all-gather.16.cloned.1.call-start = ((), (), s32[]{:S(2)}) async-start(), calls=%async_computation.14 | async-start | bytes 17825792 | tf_op jit(solution)/shard_map/all_gather | solution.py:607
  361.8 46.7 %all-to-all-start = ((bf16[16,128,264]{1,2,0:T(8,128)(2,1)}), bf16[16,128,264]{1,2,0:T(8,128)(2,1)}, u32[]{:S(2)}, u32[]{:S(2)}) async-start(bf16[16,128,264]{1,2,0:T(8,128)(2,1)} %maximum_bitcast_fusion.1), calls=%async_computation | async-start | bytes 2162688 | tf_op jit(solution)/shard_map/all_to_all | solution.py:552
  367.5 664.2 %reduce-scatter.11.cloned.1.call-start = ((), (), s32[]{:S(2)}) async-start(), calls=%async_computation.17 | async-start | bytes 17825792 | tf_op jit(solution)/shard_map/reduce_scatter | solution.py:683
  369.4 265.0 %copy-start.21 = (bf16[2048,16]{1,0:T(8,128)(2,1)}, bf16[2048,16]{1,0:T(8,128)(2,1)S(1)}, u32[]{:S(2)}) copy-start(bf16[2048,16]{1,0:T(8,128)(2,1)S(1)} %reshape.495) | copy-start | bytes 196612
  677.3 26.6 %slice-start = ((s8[9437184]{0:T(1024)(128)(4,1)}), s8[4194304]{0:T(1024)(128)(4,1)S(1)}, s32[]{:S(2)}) async-start(s8[9437184]{0:T(1024)(128)(4,1)} %bitcast.239), calls=%async_computation.26 | async-start | bytes 8388608
  677.3 26.6 %slice-start.1 = ((s8[9437184]{0:T(1024)(128)(4,1)}), s8[4194304]{0:T(1024)(128)(4,1)S(1)}, s32[]{:S(2)}) async-start(s8[9437184]{0:T(1024)(128)(4,1)} %bitcast.239), calls=%async_computation.27 | async-start | bytes 8388608
  783.7 31.6 %copy-start.13 = (bf16[2048,264]{0,1:T(8,128)(2,1)S(1)}, bf16[2048,264]{0,1:T(8,128)(2,1)}, u32[]{:S(2)}) copy-start(bf16[2048,264]{0,1:T(8,128)(2,1)} %copy_bitcast_fusion) | copy-start | bytes 3244036
  838.6 17.6 %copy-start.36 = (bf16[4096,88]{0,1:T(8,128)(2,1)}, bf16[4096,88]{0,1:T(8,128)(2,1)S(1)}, u32[]{:S(2)}) copy-start(bf16[4096,88]{0,1:T(8,128)(2,1)S(1)} %get-tuple-element.92) | copy-start | bytes 2162692
  838.6 193.2 %copy-start.26 = (bf16[4096,88]{0,1:T(8,128)(2,1)}, bf16[4096,88]{0,1:T(8,128)(2,1)S(1)}, u32[]{:S(2)}) copy-start(bf16[4096,88]{0,1:T(8,128)(2,1)S(1)} %get-tuple-element.94) | copy-start | bytes 2162692
  856.2 217.2 %all-reduce.11.cloned.1.call-start = ((), (), s32[]{:S(2)}) async-start(), calls=%async_computation.18 | async-start | bytes 2097152 | tf_op jit(solution)/shard_map/psum | solution.py:686
  1031.7 223.0 %reduce-scatter.9.cloned.1.call-start = ((), (), s32[]{:S(2)}) async-start(), calls=%async_computation.15 | async-start | bytes 17825792 | tf_op jit(solution)/shard_map/reduce_scatter | solution.py:687
  1048.7 24.7 %copy-start.3 = (bf16[256,2048]{0,1:T(8,128)(2,1)S(1)}, bf16[256,2048]{0,1:T(8,128)(2,1)}, u32[]{:S(2)}) copy-start(bf16[256,2048]{0,1:T(8,128)(2,1)} %copy.161) | copy-start | bytes 3145732
  1048.7 24.7 %copy-start.8 = (bf16[256,2048]{0,1:T(8,128)(2,1)S(1)}, bf16[256,2048]{0,1:T(8,128)(2,1)}, u32[]{:S(2)}) copy-start(bf16[256,2048]{0,1:T(8,128)(2,1)} %all-reduce.9.cloned.1.call-done) | copy-start | bytes 3145732
  1048.7 24.7 %copy-start.55 = (f32[2048]{0:T(1024)S(1)}, f32[2048]{0:T(1024)}, u32[]{:S(2)}) copy-start(f32[2048]{0:T(1024)} %copy-done.54) | copy-start | bytes 24580
  1048.8 24.7 %copy-start.64 = (f32[256]{0:T(256)S(1)}, f32[256]{0:T(256)}, u32[]{:S(2)}) copy-start(f32[256]{0:T(256)} %copy-done.63) | copy-start | bytes 3076
  1053.3 10.4 all-to-all-start.1
  1057.3 268.8 %all-reduce.17.cloned.1.call-start = ((), (), s32[]{:S(2)}) async-start(), calls=%async_computation.25 | async-start | bytes 4784128 | tf_op jit(solution)/shard_map/psum | solution.py:688
  1099.4 155.4 %copy-start.10 = (bf16[256,2048]{0,1:T(8,128)(2,1)S(1)}, bf16[256,2048]{0,1:T(8,128)(2,1)}, u32[]{:S(2)}) copy-start(bf16[256,2048]{0,1:T(8,128)(2,1)} %multiply_convert_fusion.3) | copy-start | bytes 3145732
  1254.7 179.0 %all-reduce.15.cloned.1.call-start = ((), (), s32[]{:S(2)}) async-start(), calls=%async_computation.24 | async-start | bytes 311296
  1256.2 72.2 %copy-start.12 = (f32[256,576]{0,1:T(8,128)S(1)}, f32[256,576]{0,1:T(8,128)}, u32[]{:S(2)}) copy-start(f32[256,576]{0,1:T(8,128)} %copy-done.11) | copy-start | bytes 1769476
  1256.2 72.2 %copy-start.57 = (f32[512]{0:T(512)S(1)}, f32[512]{0:T(512)}, u32[]{:S(2)}) copy-start(f32[512]{0:T(512)} %copy-done.56) | copy-start | bytes 6148
  1256.2 72.2 %copy-start.60 = (f32[256]{0:T(256)S(1)}, f32[256]{0:T(256)}, u32[]{:S(2)}) copy-start(f32[256]{0:T(256)} %copy-done.59) | copy-start | bytes 3076
  1337.2 162.9 %reduce-scatter.15.cloned.1.call-start = ((), (), s32[]{:S(2)}) async-start(), calls=%async_computation.20 | async-start | bytes 2228224 | tf_op jit(solution)/shard_map/reduce_scatter | solution.py:803
  1340.8 226.1 %reduce-scatter.19.cloned.1.call-start = ((), (), s32[]{:S(2)}) async-start(), calls=%async_computation.23 | async-start | bytes 2785280
  1347.6 294.9 %reduce-scatter.17.cloned.1.call-start = ((), (), s32[]{:S(2)}) async-start(), calls=%async_computation.21 | async-start | bytes 4456448 | tf_op jit(solution)/shard_map/reduce_scatter | solution.py:803
  1352.5 378.0 %reduce-scatter.13.cloned.1.call-start = ((), (), s32[]{:S(2)}) async-start(), calls=%async_computation.19 | async-start | bytes 6684672 | tf_op jit(solution)/shard_map/reduce_scatter | solution.py:803
  1380.8 37.9 %all-to-all-start.2 = ((bf16[16,128,264]{1,2,0:T(8,128)(2,1)}), bf16[16,128,264]{1,2,0:T(8,128)(2,1)S(1)}, u32[]{:S(2)}, u32[]{:S(2)}) async-start(bf16[16,128,264]{1,2,0:T(8,128)(2,1)} %pad_maximum_fusion.2), calls=%async_computation.7 | async-start | bytes 2162688 | tf_op jit(solution)/shard_map/all_to_all | solution.py:696
  1386.7 23.3 %slice-start.3 = ((s8[9437184]{0:T(1024)(128)(4,1)}), s8[4194304]{0:T(1024)(128)(4,1)S(1)}, s32[]{:S(2)}) async-start(s8[9437184]{0:T(1024)(128)(4,1)} %bitcast.249), calls=%async_computation.29 | async-start | bytes 8388608
  1386.7 23.3 %slice-start.4 = ((s8[9437184]{0:T(1024)(128)(4,1)}), s8[4194304]{0:T(1024)(128)(4,1)S(1)}, s32[]{:S(2)}) async-start(s8[9437184]{0:T(1024)(128)(4,1)} %bitcast.249), calls=%async_computation.30 | async-start | bytes 8388608
  1431.3 301.1 %copy-start.1 = (bf16[1,704,2048]{2,1,0:T(8,128)(2,1)S(1)}, bf16[1,704,2048]{2,1,0:T(8,128)(2,1)}, u32[]{:S(2)}) copy-start(bf16[1,704,2048]{2,1,0:T(8,128)(2,1)} %param.35) | copy-start | bytes 8650756
  (53 other events, 247.6 us)
Sparse Core Ops, SparseCore 0:
  14.2 90.3 all-reduce.12
  106.8 44.2 all-gather.7
  153.2 40.3 all-gather.9
  195.7 60.1 all-gather.11
  257.8 51.1 all-gather.13
  314.1 38.2 all-reduce.8
  354.6 149.4 all-gather.17
  506.3 128.0 all-gather.15
  856.3 175.3 reduce-scatter.10
  1033.8 39.5 all-reduce.10
  1077.6 177.1 reduce-scatter.8
  1257.5 68.5 all-reduce.16
  1337.3 96.3 all-reduce.14
  1437.3 62.7 reduce-scatter.14
  1503.8 63.1 reduce-scatter.18
  1570.7 71.7 reduce-scatter.16
  1646.3 84.1 reduce-scatter.12

commit v2 on v1

--- a/solution.py
+++ b/solution.py
@@ -1,6 +1,8 @@
 import jax
 import jax.numpy as jnp
 from jax import lax
+from jax.experimental import pallas as pl
+from jax.experimental.pallas import tpu as pltpu
 from jax.sharding import PartitionSpec as P
 
 NOPE = 128
@@ -456,25 +458,134 @@
     )
 
 
-def expert_tables(ids, expert, capacity):
+def slot_of_token(ids, expert, capacity):
     match = jnp.any(ids == expert, axis=-1)
     count = match.astype(jnp.int32)
-    place = jnp.where(match, jnp.cumsum(count, axis=-1) - count, capacity)
-    slots = jnp.arange(capacity, dtype=jnp.int32)
-    return (place[:, None, :] == slots[None, :, None]).astype(jnp.bfloat16)
-
-
-def gather_rows(table, tokens):
-    width = tokens.shape[1]
-    blocks = tokens.reshape(table.shape[0], table.shape[2], width)
-    rows = jnp.einsum("sct,std->scd", table, blocks, preferred_element_type=jnp.float32)
-    return rows.astype(jnp.bfloat16).reshape(-1, width)
-
-
-def place_rows(table, rows):
-    blocks = rows.reshape(table.shape[0], table.shape[1], -1)
-    spread = jnp.einsum("sct,scd->std", table, blocks, preferred_element_type=jnp.float32)
-    return spread.reshape(-1, spread.shape[-1])
+    return jnp.where(match, jnp.cumsum(count, axis=-1) - count, capacity)
+
+
+def pick_kernel(place_ref, *refs):
+    rows_ref = refs[-1]
+    shape = (rows_ref.shape[0], place_ref.shape[2])
+    chosen = (lax.broadcasted_iota(jnp.int32, shape, 0) == place_ref[0]).astype(jnp.bfloat16)
+    at = 0
+    for tokens_ref in refs[:-1]:
+        end = at + tokens_ref.shape[1]
+        rows_ref[:, at:end] = jnp.dot(
+            chosen, tokens_ref[...], preferred_element_type=jnp.float32
+        ).astype(jnp.bfloat16)
+        at = end
+
+
+def pick_rows(place, pieces, capacity):
+    sources, tok_count = place.shape
+    width = sum(piece.shape[1] for piece in pieces)
+    token_specs = [
+        pl.BlockSpec((tok_count, piece.shape[1]), lambda s: (s, 0)) for piece in pieces
+    ]
+    return pl.pallas_call(
+        pick_kernel,
+        grid=(sources,),
+        in_specs=[pl.BlockSpec((1, 1, tok_count), lambda s: (s, 0, 0))] + token_specs,
+        out_specs=pl.BlockSpec((capacity, width), lambda s: (s, 0)),
+        out_shape=jax.ShapeDtypeStruct((sources * capacity, width), jnp.bfloat16),
+        cost_estimate=pl.CostEstimate(
+            flops=2 * sources * capacity * tok_count * width,
+            bytes_accessed=2 * sources * (capacity + tok_count) * width,
+            transcendentals=0,
+        ),
+    )(place[:, None, :], *pieces)
+
+
+def spread_kernel(place_ref, rows_ref, scale_ref, left_ref, right_ref, *out_refs):
+    shape = (place_ref.shape[0], rows_ref.shape[0])
+    chosen = lax.broadcasted_iota(jnp.int32, shape, 1) == place_ref[...]
+    rows = (rows_ref[...].astype(jnp.float32) * scale_ref[...]).astype(jnp.bfloat16)
+    total = jnp.dot(chosen.astype(jnp.bfloat16), rows, preferred_element_type=jnp.float32)
+    total = total + jnp.dot(left_ref[...], right_ref[...], preferred_element_type=jnp.float32)
+    at = 0
+    for out_ref in out_refs:
+        end = at + out_ref.shape[0]
+        out_ref[...] = total[at:end].astype(jnp.bfloat16)
+        at = end
+
+
+def spread_rows(place, rows, scale, left, right, parts):
+    sources, tok_count = place.shape
+    capacity = rows.shape[0] // sources
+    depth, width = right.shape
+    size = tok_count // parts
+    return pl.pallas_call(
+        spread_kernel,
+        grid=(sources,),
+        in_specs=[
+            pl.BlockSpec((tok_count, 1), lambda s: (s, 0)),
+            pl.BlockSpec((capacity, width), lambda s: (s, 0)),
+            pl.BlockSpec((capacity, 1), lambda s: (s, 0)),
+            pl.BlockSpec((tok_count, depth), lambda s: (s, 0)),
+            pl.BlockSpec((depth, width), lambda s: (0, 0)),
+        ],
+        out_specs=[pl.BlockSpec((size, width), lambda s: (s, 0))] * parts,
+        out_shape=[jax.ShapeDtypeStruct((sources * size, width), jnp.bfloat16)] * parts,
+        cost_estimate=pl.CostEstimate(
+            flops=2 * sources * tok_count * width * (capacity + depth),
+            bytes_accessed=2 * sources * (capacity + tok_count) * width,
+            transcendentals=0,
+        ),
+    )(place.reshape(-1, 1), rows, scale, left, right)
+
+
+def pack_kernel(normed_ref, query_ref, down_ref, up_ref, extra_ref, out_ref):
+    contract = (((0,), (0,)), ((), ()))
+    normed = normed_ref[...]
+    query_width = query_ref.shape[1]
+    lat_part, up_width = up_ref.shape
+    up_cols = lat_part * up_width // out_ref.shape[0]
+    out_ref[:, :query_width] = lax.dot_general(
+        normed, query_ref[...], contract, preferred_element_type=jnp.float32
+    ).astype(jnp.bfloat16)
+    for index in range(up_width // up_cols):
+        out_ref[index * lat_part : (index + 1) * lat_part, query_width : query_width + up_cols] = (
+            up_ref[:, index * up_cols : (index + 1) * up_cols]
+        )
+    down = lax.dot_general(normed, down_ref[...], contract, preferred_element_type=jnp.float32)
+    out_ref[:, query_width + up_cols :] = (down + extra_ref[...].astype(jnp.float32)).astype(
+        jnp.bfloat16
+    )
+
+
+def pack_grads(normed, query_grad, down_grad, up_grad, extra, dp_count):
+    tok_count, width = normed.shape
+    d_part = width // dp_count
+    lat_part = up_grad.shape[0] // dp_count
+    up_cols = lat_part * up_grad.shape[1] // d_part
+    total = query_grad.shape[1] + up_cols + down_grad.shape[1]
+    return pl.pallas_call(
+        pack_kernel,
+        grid=(dp_count,),
+        in_specs=[
+            pl.BlockSpec((tok_count, d_part), lambda d: (0, d)),
+            pl.BlockSpec(query_grad.shape, lambda d: (0, 0)),
+            pl.BlockSpec(down_grad.shape, lambda d: (0, 0)),
+            pl.BlockSpec((lat_part, up_grad.shape[1]), lambda d: (d, 0)),
+            pl.BlockSpec((d_part, extra.shape[1]), lambda d: (d, 0)),
+        ],
+        out_specs=pl.BlockSpec((d_part, total), lambda d: (d, 0)),
+        out_shape=jax.ShapeDtypeStruct((width, total), jnp.bfloat16),
+        cost_estimate=pl.CostEstimate(
+            flops=2 * tok_count * width * (query_grad.shape[1] + down_grad.shape[1]),
+            bytes_accessed=3 * width * total,
+            transcendentals=0,
+        ),
+    )(normed, query_grad, down_grad, up_grad, extra)
+
+
+def sum_tensor(part):
+    if lax.axis_size("tensor") != 2:
+        return lax.psum(part, "tensor").astype(jnp.float32)
+    part = lax.optimization_barrier(part)
+    other = lax.ppermute(part, "tensor", [(0, 1), (1, 0)])
+    return part.astype(jnp.float32) + other.astype(jnp.float32)
 
 
 def local_gathered(
@@ -514,33 +625,19 @@
     lat_part = latent_up.shape[0]
     hid_slice = shared_gate.shape[1] // dp_count
 
-    small = jnp.concatenate(
-        [
-            attn_gain,
-            ffn_gain,
-            latent_gain,
-            router_weight.reshape(-1),
-            expert_ids.T.reshape(-1).astype(low_type),
-        ]
-    )
-    small_all = lax.all_gather(small, "dp", axis=0, tiled=False)
-    cuts = [d_part, d_part, lat_part, d_part * num_experts, tok_count * top_count]
-    pieces, at = [], 0
-    for size in cuts:
-        pieces.append(small_all[:, at : at + size])
-        at += size
-    full_attn_gain = pieces[0].reshape(-1).astype(float_type)
-    full_ffn_gain = pieces[1].reshape(-1).astype(float_type)
-    full_lgain = pieces[2].reshape(-1).astype(float_type)
-    full_router = pieces[3].reshape(width, num_experts)
-    ids_all = jnp.transpose(
-        pieces[4].reshape(dp_count, top_count, tok_count).astype(jnp.int32), (0, 2, 1)
-    )
-    full_query = lax.all_gather(query_proj, "dp", axis=0, tiled=True)
-    full_down = lax.all_gather(latent_down, "dp", axis=0, tiled=True)
-    full_up = lax.all_gather(latent_up, "dp", axis=0, tiled=True)
-    full_output_t = lax.all_gather(output_proj.T, "dp", axis=0, tiled=True)
-
+    lgain_cols = -(-lat_part // d_part)
+    gate_columns = jnp.pad(latent_gain, (0, lgain_cols * d_part - lat_part))
+    small_columns = [
+        attn_gain.reshape(d_part, 1),
+        ffn_gain.reshape(d_part, 1),
+        gate_columns.reshape(d_part, lgain_cols),
+        router_weight,
+        expert_ids.T.reshape(d_part, -1).astype(low_type),
+    ]
+    big_columns = [query_proj, latent_up.reshape(d_part, -1), latent_down]
+    packed = jnp.concatenate(big_columns + small_columns, axis=1)
+    packed = jnp.pad(packed, ((0, 0), (0, -packed.shape[1] % 128)))
+    packed_all = lax.all_gather(packed, "dp", axis=0, tiled=True)
     shared_send = jnp.concatenate(
         [
             shared_gate.reshape(d_part, dp_count, hid_slice),
@@ -552,9 +649,26 @@
     shared_mine = lax.all_to_all(
         jnp.transpose(shared_send, (1, 0, 2)), "dp", split_axis=0, concat_axis=0, tiled=True
     ).reshape(width, 3 * hid_slice)
+    cut = width // 512 * 128
+    packed_all, shared_mine, output_part = lax.optimization_barrier(
+        (packed_all, shared_mine, output_proj.T)
+    )
+    full_output_t = lax.all_gather(output_part, "dp", axis=0, tiled=True)
+    pieces, at = [], 0
+    for columns in big_columns + small_columns:
+        pieces.append(packed_all[:, at : at + columns.shape[1]])
+        at += columns.shape[1]
+    full_query, full_up, full_down = pieces[:3]
+    full_up = full_up.reshape(-1, latent_up.shape[1])
+    full_attn_gain = pieces[3].reshape(-1).astype(float_type)
+    full_ffn_gain = pieces[4].reshape(-1).astype(float_type)
+    full_lgain = pieces[5].reshape(dp_count, -1)[:, :lat_part].reshape(-1).astype(float_type)
+    full_router = pieces[6]
+    ids_all = jnp.transpose(
+        pieces[7].reshape(dp_count, top_count, tok_count).astype(jnp.int32), (0, 2, 1)
+    )
     gate_up_w = shared_mine[:, : 2 * hid_slice]
     down_w_t = shared_mine[:, 2 * hid_slice :]
-    grad_all = lax.all_gather(grad_out, "dp", axis=0, tiled=True)
 
     def by_seq(array):
         return array.reshape((seq_count, seq_len) + array.shape[1:])
@@ -573,6 +687,8 @@
         [query_raw[..., :NOPE], rotate(query_raw[..., NOPE:], cos_tok[:, None], sin_tok[:, None])],
         axis=-1,
     ).astype(low_type)
+    queries, first_columns = lax.optimization_barrier((queries, grad_out[:, :cut]))
+    grad_first = lax.all_gather(first_columns, "dp", axis=0, tiled=True)
     down_raw = jnp.dot(normed_one, full_down, preferred_element_type=float_type)
     latent = down_raw[:, :LAT]
     recip_latent = rms_recip(latent)
@@ -600,11 +716,13 @@
     attn_part = lax.dot_general(
         attn_flat, full_output_t, (((1,), (1,)), ((), ())), preferred_element_type=float_type
     )
-    attn_full = lax.psum(attn_part.astype(low_type), "tensor").astype(float_type)
+    attn_full = sum_tensor(attn_part.astype(low_type))
     mid = residual_in + attn_full
     recip_two = rms_recip(mid)
     normed_two = (mid * recip_two * full_ffn_gain).astype(low_type)
     tok_all = lax.all_gather(normed_two, "dp", axis=0, tiled=True)
+    tok_all, other_columns = lax.optimization_barrier((tok_all, grad_out[:, cut:]))
+    grad_other = lax.all_gather(other_columns, "dp", axis=0, tiled=True)
 
     logits_all = jnp.dot(tok_all, full_router, preferred_element_type=float_type)
     probs_all = jax.nn.softmax(logits_all, axis=-1)
@@ -616,41 +734,77 @@
     shared_pre_up = pre_all[:, hid_slice:]
     shared_act, shared_slope = silu_parts(pre_all[:, :hid_slice])
     shared_hidden = (shared_act * shared_pre_up).astype(low_type)
-    shared_act_grad = jnp.dot(grad_all, down_w_t, preferred_element_type=float_type)
+    split = 2 if lax.axis_size("tensor") == 2 else 1
+    turn = lax.axis_index("tensor") if split == 2 else 0
+
+    def own_half_first(array):
+        if split == 1:
+            return array
+        halves = array.reshape((dp_count, 2, tok_count // 2) + array.shape[1:])
+        return jnp.where(turn == 0, halves, halves[:, ::-1]).reshape(array.shape)
+
+    ffn_parts, in_grad_part = None, None
+    saved = []
+    for index in range(local_experts):
+        expert = my_dp * local_experts + index
+        place = slot_of_token(ids_all, expert, capacity)
+        slots = jnp.arange(capacity, dtype=jnp.int32)
+        table = place[:, None, :] == slots[None, :, None]
+        token_rows = pick_rows(place, [tok_all], capacity)
+        column = jnp.sum(
+            jnp.where(jnp.arange(num_experts, dtype=jnp.int32) == expert, probs_all, 0.0), axis=-1
+        ).reshape(dp_count, 1, tok_count)
+        gate_of = jnp.sum(jnp.where(table, column, 0.0), axis=-1).reshape(-1, 1)
+        pre_gate = jnp.dot(token_rows, routed_gate_weight[index], preferred_element_type=float_type)
+        pre_up = jnp.dot(token_rows, routed_up_weight[index], preferred_element_type=float_type)
+        expert_act, expert_slope = silu_parts(pre_gate)
+        expert_hidden = (expert_act * pre_up).astype(low_type)
+        expert_result = jnp.dot(
+            expert_hidden, routed_down_weight[index], preferred_element_type=float_type
+        ).astype(low_type)
+        left = shared_hidden if index == 0 else jnp.zeros_like(shared_hidden)
+        addends = spread_rows(
+            own_half_first(place.reshape(-1)).reshape(place.shape),
+            expert_result,
+            gate_of,
+            own_half_first(left),
+            down_w_t.T,
+            split,
+        )
+        ffn_parts = addends if index == 0 else [a + b for a, b in zip(ffn_parts, addends)]
+        saved.append(
+            (place, table, token_rows, gate_of, pre_up, expert_act, expert_slope, expert_hidden)
+            + (expert_result,)
+        )
+    grad_first, grad_other, ffn_parts = lax.optimization_barrier(
+        (grad_first, grad_other, ffn_parts)
+    )
+    if split == 2:
+        from_other = lax.ppermute(ffn_parts[1], "tensor", [(0, 1), (1, 0)])
+        ffn_half = (ffn_parts[0].astype(float_type) + from_other.astype(float_type)).astype(
+            low_type
+        )
+    else:
+        ffn_half = ffn_parts[0]
+
+    shared_act_grad = jnp.dot(
+        grad_first, down_w_t[:cut], preferred_element_type=float_type
+    ) + jnp.dot(grad_other, down_w_t[cut:], preferred_element_type=float_type)
     shared_grads = jnp.concatenate(
         [shared_act_grad * shared_pre_up * shared_slope, shared_act_grad * shared_act], axis=-1
     ).astype(low_type)
-    ffn_part = lax.dot_general(
-        shared_hidden, down_w_t, (((1,), (1,)), ((), ())), preferred_element_type=float_type
-    )
-    in_grad_part = lax.dot_general(
-        shared_grads, gate_up_w, (((1,), (1,)), ((), ())), preferred_element_type=float_type
-    )
 
     expert_columns, routed_grads = [], []
     for index in range(local_experts):
-        expert = my_dp * local_experts + index
         gate_w = routed_gate_weight[index]
         up_w = routed_up_weight[index]
         down_w = routed_down_weight[index]
-        table = expert_tables(ids_all, expert, capacity)
-        token_rows = gather_rows(table, tok_all)
-        grad_rows = gather_rows(table, grad_all).astype(float_type)
-        column = jnp.sum(
-            jnp.where(jnp.arange(num_experts, dtype=jnp.int32) == expert, probs_all, 0.0), axis=-1
-        ).reshape(dp_count, 1, tok_count)
-        gate_of = jnp.sum(table.astype(float_type) * column, axis=-1).reshape(-1, 1)
-        pre_gate = jnp.dot(token_rows, gate_w, preferred_element_type=float_type)
-        pre_up = jnp.dot(token_rows, up_w, preferred_element_type=float_type)
-        expert_act, expert_slope = silu_parts(pre_gate)
-        expert_hidden = (expert_act * pre_up).astype(low_type)
-        expert_result = jnp.dot(expert_hidden, down_w, preferred_element_type=float_type).astype(
-            low_type
-        )
-        result_float = expert_result.astype(float_type)
-        weight_rows = jnp.sum(grad_rows * result_float, axis=-1).reshape(dp_count, capacity, 1)
-        expert_columns.append(jnp.sum(table.astype(float_type) * weight_rows, axis=1))
-        ffn_part = ffn_part + place_rows(table, (gate_of * result_float).astype(low_type))
+        place, table, token_rows, gate_of, pre_up, expert_act, expert_slope = saved[index][:7]
+        expert_hidden, expert_result = saved[index][7:]
+        grad_rows = pick_rows(place, [grad_first, grad_other], capacity).astype(float_type)
+        weight_rows = jnp.sum(grad_rows * expert_result.astype(float_type), axis=-1)
+        weight_rows = weight_rows.reshape(dp_count, capacity, 1)
+        expert_columns.append(jnp.sum(jnp.where(table, weight_rows, 0.0), axis=1))
         slot_grad = (gate_of * grad_rows).astype(low_type)
         hidden_grad = lax.dot_general(
             slot_grad, down_w, (((1,), (1,)), ((), ())), preferred_element_type=float_type
@@ -663,7 +817,11 @@
         row_grad = row_grad + lax.dot_general(
             pre_up_grad, up_w, (((1,), (1,)), ((), ())), preferred_element_type=float_type
         )
-        in_grad_part = in_grad_part + place_rows(table, row_grad.astype(low_type))
+        left = shared_grads if index == 0 else jnp.zeros_like(shared_grads)
+        addend = spread_rows(
+            place, row_grad.astype(low_type), jnp.ones_like(gate_of), left, gate_up_w.T, 1
+        )[0]
+        in_grad_part = addend if index == 0 else in_grad_part + addend
         routed_grads.append(
             (
                 jnp.dot(token_rows.T, pre_gate_grad, preferred_element_type=float_type),
@@ -679,20 +837,24 @@
             num_experts, tok_count
         )
     )
-    prob_grad = lax.psum(prob_part, "tensor")
-    in_grad = lax.psum_scatter(
-        in_grad_part.astype(low_type), "dp", scatter_dimension=0, tiled=True
-    )
-    normed_two_grad = lax.psum(in_grad, "tensor").astype(float_type)
-    ffn_sum = lax.psum_scatter(ffn_part.astype(low_type), "dp", scatter_dimension=0, tiled=True)
-    ffn_full = lax.psum(ffn_sum, "tensor").astype(float_type)
-    output = (mid + ffn_full).astype(low_type)
-
+    prob_grad = sum_tensor(prob_part)
+    in_grad = lax.psum_scatter(in_grad_part, "dp", scatter_dimension=0, tiled=True)
     shared_gate_up_grad = jnp.dot(tok_all.T, shared_grads, preferred_element_type=float_type)
-    shared_down_grad_t = jnp.dot(grad_all.T, shared_hidden, preferred_element_type=float_type)
+    shared_down_grad_t = jnp.concatenate(
+        [
+            jnp.dot(grad_first.T, shared_hidden, preferred_element_type=float_type),
+            jnp.dot(grad_other.T, shared_hidden, preferred_element_type=float_type),
+        ],
+        axis=0,
+    )
     shared_back = jnp.concatenate([shared_gate_up_grad, shared_down_grad_t], axis=-1).astype(
         low_type
     )
+    in_grad, prob_grad, shared_back, routed_out, ffn_half = lax.optimization_barrier(
+        (in_grad, prob_grad, shared_back, routed_out, ffn_half)
+    )
+    normed_two_grad = sum_tensor(in_grad)
+    ffn_sum = lax.psum_scatter(ffn_half, "dp", scatter_dimension=0, tiled=True)
     shared_back = lax.all_to_all(
         shared_back.reshape(dp_count, d_part, 3 * hid_slice),
         "dp",
@@ -762,9 +924,6 @@
         .astype(low_type)
         .reshape(tok_count, head_count * head_dim)
     )
-    query_projection_gradient = jnp.dot(
-        normed_one.T, query_raw_grad, preferred_element_type=float_type
-    )
     kv_grad = (
         jnp.concatenate([key_nope_grad, values_grad], axis=-1)
         .astype(low_type)
@@ -781,7 +940,7 @@
     parts = jnp.concatenate(
         [normed_one_part, latent_part_grad, rope_part_grad], axis=-1
     ).astype(low_type)
-    sums = lax.psum(parts, "tensor").astype(float_type)
+    sums = sum_tensor(parts)
     normed_one_grad = sums[:, :width]
     latent_normed_grad = sums[:, width : width + LAT]
     rope_key_grad = sums[:, width + LAT :]
@@ -790,7 +949,6 @@
     )
     rope_pre_grad = rotate(rope_key_grad, cos_tok, -sin_tok)
     down_grad = jnp.concatenate([latent_grad, rope_pre_grad], axis=-1).astype(low_type)
-    latent_down_gradient = jnp.dot(normed_one.T, down_grad, preferred_element_type=float_type)
     normed_one_grad = normed_one_grad + lax.dot_general(
         down_grad, full_down, (((1,), (1,)), ((), ())), preferred_element_type=float_type
     )
@@ -804,28 +962,67 @@
             array.astype(low_type), "dp", scatter_dimension=0, tiled=True
         ).astype(float_type)
 
-    small_grads = jnp.concatenate(
-        [
-            attention_gain_gradient.reshape(dp_count, -1),
-            feedforward_gain_gradient.reshape(dp_count, -1),
-            latent_gain_gradient.reshape(dp_count, -1),
-            router_weight_gradient.reshape(dp_count, -1),
-        ],
-        axis=-1,
-    )
-    small_sums = lax.psum_scatter(small_grads, "dp", scatter_dimension=0, tiled=True).reshape(-1)
-    one, two, three = d_part, 2 * d_part, 2 * d_part + lat_part
+    lgain_grad = jnp.pad(
+        latent_gain_gradient.reshape(dp_count, lat_part),
+        ((0, 0), (0, lgain_cols * d_part - lat_part)),
+    )
+    columns = [
+        attention_gain_gradient.reshape(width, 1),
+        feedforward_gain_gradient.reshape(width, 1),
+        lgain_grad.reshape(width, lgain_cols),
+        router_weight_gradient,
+    ]
+    small_grads = jnp.concatenate([array.astype(low_type) for array in columns], axis=1)
+    down_width = down_grad.shape[1]
+    spare = -(down_width + small_grads.shape[1]) % 128
+    small_grads = jnp.pad(small_grads, ((0, 0), (down_width, spare)))
+    wide_down_grad = jnp.pad(down_grad, ((0, 0), (0, small_grads.shape[1] - down_width)))
+    packed_grads = pack_grads(
+        normed_one,
+        query_raw_grad,
+        wide_down_grad,
+        latent_up_gradient.astype(low_type),
+        small_grads,
+        dp_count,
+    )
+    output_sums = lax.psum_scatter(
+        output_projection_gradient_t.astype(low_type), "dp", scatter_dimension=0, tiled=True
+    )
+    packed_grads, ffn_sum, output_sums = lax.optimization_barrier(
+        (packed_grads, ffn_sum, output_sums)
+    )
+    packed_sums = scatter(packed_grads)
+    if split == 2:
+        ffn_other = lax.ppermute(ffn_sum, "tensor", [(0, 1), (1, 0)])
+        ffn_full = jnp.where(
+            turn == 0,
+            jnp.concatenate([ffn_sum, ffn_other], axis=0),
+            jnp.concatenate([ffn_other, ffn_sum], axis=0),
+        ).astype(float_type)
+    else:
+        ffn_full = sum_tensor(ffn_sum)
+    output = (mid + ffn_full).astype(low_type)
+    query_width = query_raw_grad.shape[1]
+    up_cols = lat_part * latent_up.shape[1] // d_part
+    up_sums = packed_sums[:, query_width : query_width + up_cols]
+    up_sums = jnp.transpose(up_sums.reshape(-1, lat_part, up_cols), (1, 0, 2))
+    at = query_width + up_cols
+    down_sums = packed_sums[:, at : at + down_width]
+    sums_of, at = [], at + down_width
+    for array in columns:
+        sums_of.append(packed_sums[:, at : at + array.shape[1]])
+        at += array.shape[1]
     return (
         output,
         hidden_input_gradient,
-        small_sums[:one],
-        scatter(query_projection_gradient),
-        scatter(latent_down_gradient),
-        small_sums[two:three],
-        scatter(latent_up_gradient),
-        scatter(output_projection_gradient_t).T,
-        small_sums[one:two],
-        small_sums[three:].reshape(d_part, num_experts),
+        sums_of[0].reshape(-1),
+        packed_sums[:, :query_width],
+        down_sums,
+        sums_of[2].reshape(-1)[:lat_part],
+        up_sums.reshape(lat_part, -1),
+        output_sums.astype(float_type).T,
+        sums_of[1].reshape(-1),
+        sums_of[3],
         shared_gate_gradient,
         shared_up_gradient,
         shared_down_gradient,

time: 1750 us -> 1160 us (0.66)
  waiting for transfers between devices: 1180 us -> 581 us
  matrix products: 313 us -> 202 us
  Pallas kernels: 0 us -> 88.1 us
  blocking collectives: 8.92 us -> 88.9 us
  local copies, waits for them, and re-layouts: 150 us -> 91.8 us
    ppermute x0 -> x6, waiting for transfers between devices: none -> 191 us  [the longest x4 184 us: sum_tensor(): other = lax.ppermute(part, 'tensor', [(0, 1), (1, 0)])]
    reduce_scatter x2 -> x3, waiting for transfers between devices: 261 us -> 84 us  [the longest x1 84 us: local_gathered(): ffn_sum = lax.psum_scatter(ffn_half, 'dp', scatter_dimension=0, tiled=True)]
    all_gather x5 -> x4, waiting for transfers between devices: 275 us -> 110 us  [the longest x1 53.8 us: local_gathered(): packed_all = lax.all_gather(packed, 'dp', axis=0, tiled=True)]
    unnamed x20 -> x9, waiting for transfers between devices: 151 us -> 1.33 us
    reduce_scatter x3 -> x1, waiting for transfers between devices: 220 us -> 72.2 us  [scatter(): lax.psum_scatter(array.astype(low_type), 'dp', scatter_dimension=0, tiled...]
    dot_general x13 -> x7, matrix products: 162 us -> 55.2 us  [the longest x1 10.7 us: local_gathered(): jnp.dot(token_rows, routed_up_weight[index], preferred_element_type=float...]
    psum x3 -> x0, waiting for transfers between devices: 106 us -> none  [the longest x1 68 us: local_gathered(): ffn_full = lax.psum(ffn_sum, 'tensor').astype(float_type)]
    all_to_all x0 -> x2, blocking collectives: none -> 88.9 us  [the longest x1 56.9 us: local_gathered(): lax.all_to_all(jnp.transpose(shared_send, (1, 0, 2)), 'dp', split_axis=0,...]
  transfers between devices with their start and end apart: 20 -> 16, of which waited for: 18 -> 11; matrix products, arithmetic and copies ran while one was open for 15% -> 22% of each run, Pallas kernels for 0% -> 4%
where the time goes in v2:
time: 1160 us; the launch traced here: 1140 us
  waiting for transfers between devices  581 us (50%)
  matrix products  202 us (17%)
  local copies, waits for them, and re-layouts  91.8 us (8%)
  blocking collectives  88.9 us (8%)
  Pallas kernels  88.1 us (8%)
  other arithmetic  62.3 us (5%)
  between operations  15.5 us (1%)
  starting transfers between devices  12.4 us (1%)
    ppermute x4, waiting for transfers between devices, sum_tensor(): other = lax.ppermute(part, 'tensor', [(0, 1), (1, 0)])  184 us
    all_gather x1, waiting for transfers between devices, local_gathered(): tok_all = lax.all_gather(normed_two, 'dp', axis=0, tiled=True)  122 us
    reduce_scatter x1, waiting for transfers between devices, local_gathered(): ffn_sum = lax.psum_scatter(ffn_half, 'dp', scatter_dimension=0, tiled=True)  84 us
    reduce_scatter x1, waiting for transfers between devices, scatter(): lax.psum_scatter(array.astype(low_type), 'dp', scatter_dimension=0, tiled...  72.2 us
    all_to_all x1, blocking collectives, local_gathered(): lax.all_to_all(jnp.transpose(shared_send, (1, 0, 2)), 'dp', split_axis=0,...  56.9 us
    all_gather x1, waiting for transfers between devices, local_gathered(): packed_all = lax.all_gather(packed, 'dp', axis=0, tiled=True)  53.8 us
    all_gather x1, waiting for transfers between devices, local_gathered(): grad_other = lax.all_gather(other_columns, 'dp', axis=0, tiled=True)  46 us
    pallas_call x2, Pallas kernels, spread_rows(): pl.pallas_call(spread_kernel, grid=(sources,), in_specs=[pl.BlockSpec((to...  39.9 us
  transfers between devices with their start and end apart: 16, of which 11 were waited for; matrix products, arithmetic and copies ran while one was open for 22% of the time, Pallas kernels for 4%

profile of v2, /device:TPU:0, one launch (start us, length us, event | category | flops | bytes accessed | tf_op | source)
XLA Modules:
  0.0 1142.3 jit_solution(12791113167947920865)
XLA Ops:
  21.7 56.9 %all_to_all.15 = bf16[16,128,264]{1,2,0:T(8,128)(2,1)S(1)} all-to-all(bf16[16,128,264]{1,2,0:T(8,128)(2,1)S(1)} %maximum_bitcast_fusion.1), channel_id=1, replica_groups=mesh['dp'=16,'tensor'=2] {'dp'}, dimensions={0} | all-to-all | bytes 2162688 | tf_op jit(solution)/shard_map/all_to_all | solution.py:649
  79.7 53.8 %all-gather.6.cloned.1.call-done = bf16[2048,2688]{1,0:T(8,128)(2,1)} async-done(((bf16[128,2688]{1,0:T(8,128)(2,1)}), bf16[2048,2688]{1,0:T(8,128)(2,1)}) %all-gather.6.cloned.1.call-update) | async-done | bytes 11010064 | tf_op jit(solution)/shard_map/all_gather | solution.py:640
  137.5 3.1 slice.174
  143.0 3.1 fusion.32
  151.6 5.8 fusion.5
  161.4 4.4 reshape.571
  175.8 10.6 all-gather.8.cloned.1.call-done
  186.4 3.5 convolution_convert_fusion.4
  191.5 23.8 %collective-permute-done = bf16[256,2048]{1,0:T(8,128)(2,1)S(1)} collective-permute-done((bf16[256,2048]{1,0:T(8,128)(2,1)S(1)}, bf16[256,2048]{1,0:T(8,128)(2,1)S(1)}, u32[]{:S(2)}, u32[]{:S(2)}) %collective-permute-start) | collective-permute-done | bytes 1048608 | tf_op jit(solution)/shard_map/ppermute | solution.py:587
  221.4 122.0 %all-gather.10.cloned.1.call-done.refs_0_ = bf16[4096,2048]{1,0:T(8,128)(2,1)} async-done(((bf16[256,2048]{1,0:T(8,128)(2,1)}), bf16[4096,2048]{1,0:T(8,128)(2,1)}) %all-gather.10.cloned.1.call-update) | async-done | bytes 16777232 | tf_op jit(solution)/shard_map/all_gather | solution.py:723
  358.1 10.4 fusion.93
  370.9 16.3 %shard_map.297 = bf16[2304,2048]{1,0:T(8,128)(2,1)} custom-call(s32[16,1,256]{2,1,0:T(1,128)} %copy_select_fusion.place_ref, bf16[4096,2048]{1,0:T(8,128)(2,1)} %all-gather.10.cloned.1.call-done.refs_0_), custom_call_target="tpu_custom_call" | custom-call | flops 2415919104 | bytes 26214400 | tf_op jit(solution)/shard_map/pallas_call | solution.py:486
  387.3 8.7 fusion.50
  400.4 9.3 fusion.25
  409.7 10.7 multiply_convert_fusion.2
  420.4 9.7 convolution_convert_fusion.rows_ref
  430.1 19.5 %shard_map.298 = (bf16[2048,2048]{1,0:T(8,128)(2,1)}, bf16[2048,2048]{1,0:T(8,128)(2,1)}) custom-call(s32[4096,1]{1,0:T(8,128)} %copy.404.place_ref, bf16[2304,2048]{1,0:T(8,128)(2,1)} %convolution_convert_fusion.rows_ref, f32[2304,1]{1,0:T(8,128)} %reshape.603.scale_ref, bf16[4096,88]{1,0:T(8,128)(2,1)} %bitcast.259, ...), custom_call_target="tpu_custom_call" | custom-call | flops 3892314112 | bytes 26214400 | tf_op jit(solution)/shard_map/pallas_call | solution.py:518
  449.6 46.0 %all-gather.14.cloned.1.call-done.refs_1_ = bf16[4096,1536]{1,0:T(8,128)(2,1)} async-done(((bf16[256,1536]{1,0:T(8,128)(2,1)}), bf16[4096,1536]{1,0:T(8,128)(2,1)}) %all-gather.14.cloned.1.call-update) | async-done | bytes 12582928 | tf_op jit(solution)/shard_map/all_gather | solution.py:725
  495.6 9.3 fusion.70
  504.9 16.4 %shard_map.299 = bf16[2304,2048]{1,0:T(8,128)(2,1)} custom-call(s32[16,1,256]{2,1,0:T(1,128)} %copy_select_fusion.place_ref, bf16[4096,512]{1,0:T(8,128)(2,1)} %all-gather.12.cloned.1.call-done.refs_0_, bf16[4096,1536]{1,0:T(8,128)(2,1)} %all-gather.14.cloned.1.call-done.refs_1_), custom_call_target="tpu_custom_call" | custom-call | flops 2415919104 | bytes 26214400 | tf_op jit(solution)/shard_map/pallas_call | solution.py:486
  521.3 6.1 multiply_convert_fusion.4
  529.2 12.9 %multiply_convert_fusion = (bf16[2304,704]{0,1:T(8,128)(2,1)}, bf16[2304,704]{0,1:T(8,128)(2,1)}) fusion(f32[2304,704]{0,1:T(8,128)} %fusion.25, f32[2304,704]{0,1:T(8,128)} %get-tuple-element.196, bf16[1,704,2048]{2,1,0:T(8,128)(2,1)S(1)} %copy-done, bf16[2304,2048]{1,0:T(8,128)(2,1)S(1)} %copy-done.6, f32[2304]{0:T(1024)S(1)} %mul.325), kind=kOutput, calls=%fused_computation.7 | convolution fusion | flops 6679019520 | bytes 31794176 | tf_op jit(solution)/shard_map/dot_general | solution.py:809
  542.1 13.9 %fusion.23 = f32[2304,2048]{1,0:T(8,128)} fusion(bf16[2304,704]{0,1:T(8,128)(2,1)} %get-tuple-element.173, bf16[1,2048,704]{1,2,0:T(8,128)(2,1)} %param.33), kind=kOutput, calls=%fused_computation.36 | convolution fusion | flops 6643777536 | bytes 25001984 | tf_op jit(solution)/shard_map/dot_general | solution.py:814
  558.2 14.5 %add_convert_fusion.rows_ref = bf16[2304,2048]{1,0:T(8,128)(2,1)} fusion(f32[2304,2048]{1,0:T(8,128)} %fusion.23, bf16[2304,704]{0,1:T(8,128)(2,1)S(1)} %copy-done.75, bf16[1,2048,704]{1,2,0:T(8,128)(2,1)S(1)} %copy-done.73), kind=kOutput, calls=%fused_computation.4 | convolution fusion | flops 6653214720 | bytes 34439168 | tf_op jit(solution)/shard_map/dot_general | solution.py:817
  573.8 20.3 %shard_map.300 = bf16[4096,2048]{1,0:T(8,128)(2,1)} custom-call(s32[4096,1]{1,0:T(8,128)} %subtract_select_fusion.place_ref, bf16[2304,2048]{1,0:T(8,128)(2,1)} %add_convert_fusion.rows_ref, f32[2304,1]{1,0:T(8,128)} %broadcast_in_dim.101.scale_ref, bf16[4096,176]{1,0:T(8,128)(2,1)} %pad_maximum_fusion.left_ref, bf16[176,2048]{1,0:T(8,128)(2,1)} %slice_bitcast_fusion.right_ref), custom_call_target="tpu_custom_call" | custom-call | flops 5368709120 | bytes 26214400 | tf_op jit(solution)/shard_map/pallas_call | solution.py:518
  595.7 11.1 fusion.1
  608.0 3.5 all-to-all-start.1
  611.6 9.3 convolution_convert_fusion.6
  620.9 9.4 convolution_convert_fusion.5
  630.4 9.0 convolution_bitcast_fusion
  639.4 8.7 convolution_bitcast_fusion.1
  648.2 8.9 fusion.11
  659.5 118.0 %collective-permute-done.1 = f32[256,16]{0,1:T(8,128)S(1)} collective-permute-done((f32[256,16]{0,1:T(8,128)S(1)}, f32[256,16]{0,1:T(8,128)S(1)}, u32[]{:S(2)}, u32[]{:S(2)}) %collective-permute-start.1) | collective-permute-done | bytes 16416 | tf_op jit(solution)/shard_map/ppermute | solution.py:587
  777.5 10.7 add_convert_fusion.1
  791.7 21.2 %collective-permute-done.3 = bf16[256,2048]{1,0:T(8,128)(2,1)S(1)} collective-permute-done((bf16[256,2048]{1,0:T(8,128)(2,1)}, bf16[256,2048]{1,0:T(8,128)(2,1)S(1)}, u32[]{:S(2)}, u32[]{:S(2)}) %collective-permute-start.3) | collective-permute-done | bytes 1048608 | tf_op jit(solution)/shard_map/ppermute | solution.py:587
  813.0 2.7 multiply_reduce_fusion
  817.7 3.4 convolution_convert_fusion.1
  822.1 4.9 convolution_convert_fusion.9
  847.0 5.2 fusion.27
  861.5 3.5 convolution_convert_fusion.2.up_ref
  865.0 20.9 %collective-permute-done.4 = bf16[256,2624]{0,1:T(8,128)(2,1)} collective-permute-done((bf16[256,2624]{0,1:T(8,128)(2,1)}, bf16[256,2624]{0,1:T(8,128)(2,1)}, u32[]{:S(2)}, u32[]{:S(2)}) %collective-permute-start.4) | collective-permute-done | bytes 1343520 | tf_op jit(solution)/shard_map/ppermute | solution.py:587
  891.8 4.3 fusion.36
  899.2 15.5 %shard_map.301 = bf16[2048,2688]{1,0:T(8,128)(2,1)} custom-call(bf16[256,2048]{1,0:T(8,128)(2,1)} %copy-done.32, bf16[256,1536]{1,0:T(8,128)(2,1)} %copy.426.query_ref, bf16[256,640]{1,0:T(8,128)(2,1)} %pad.23.down_ref, bf16[512,2048]{1,0:T(8,128)(2,1)} %convolution_convert_fusion.2.up_ref, bf16[2048,640]{1,0:T(8,128)(2,1)} %pad.25.extra_ref), custom_call_target="tpu_custom_call" | custom-call | flops 2281701376 | bytes 16515072 | tf_op jit(solution)/shard_map/pallas_call | solution.py:563
  914.7 84.0 %reduce-scatter.7.cloned.1.call-done = bf16[128,2048]{1,0:T(8,128)(2,1)} async-done(((bf16[2048,2048]{1,0:T(8,128)(2,1)}), bf16[128,2048]{1,0:T(8,128)(2,1)}) %reduce-scatter.7.cloned.1.call-update) | async-done | bytes 524304 | tf_op jit(solution)/shard_map/reduce_scatter | solution.py:857
  1000.2 32.0 %all_to_all.16 = bf16[16,128,264]{1,2,0:T(8,128)(2,1)S(1)} all-to-all(bf16[16,128,264]{1,2,0:T(8,128)(2,1)S(1)} %copy_bitcast_fusion.1), channel_id=1, replica_groups=mesh['dp'=16,'tensor'=2] {'dp'}, dimensions={0} | all-to-all | bytes 2162688 | tf_op jit(solution)/shard_map/all_to_all | solution.py:858
  1038.5 4.5 fusion.39
  1044.0 7.1 collective-permute-done.5
  1053.7 72.2 %reduce-scatter.11.cloned.1.call-done = bf16[128,2688]{1,0:T(8,128)(2,1)} async-done(((bf16[2048,2688]{1,0:T(8,128)(2,1)}), bf16[128,2688]{1,0:T(8,128)(2,1)}) %reduce-scatter.11.cloned.1.call-update) | async-done | bytes 688144 | tf_op jit(solution)/shard_map/reduce_scatter | solution.py:961
  (352 shorter events, 145.7 us)
Async XLA Ops:
  7.2 413.2 %copy-start = (bf16[1,704,2048]{2,1,0:T(8,128)(2,1)S(1)}, bf16[1,704,2048]{2,1,0:T(8,128)(2,1)}, u32[]{:S(2)}) copy-start(bf16[1,704,2048]{2,1,0:T(8,128)(2,1)} %param.35) | copy-start | bytes 8650756
  7.2 126.3 %all-gather.6.cloned.1.call-start = ((), (), s32[]{:S(2)}) async-start(), calls=%async_computation.7 | async-start | bytes 11698176 | tf_op jit(solution)/shard_map/all_gather | solution.py:640
  17.4 169.1 %all-gather.8.cloned.1.call-start = ((), (), s32[]{:S(2)}) async-start(), calls=%async_computation.8 | async-start | bytes 4456448 | tf_op jit(solution)/shard_map/all_gather | solution.py:656
  78.5 58.2 %copy-start.70 = (s32[1,256]{1,0:T(1,128)S(1)}, s32[1,256]{1,0:T(1,128)}, u32[]{:S(2)}) copy-start(s32[1,256]{1,0:T(1,128)} %param.19) | copy-start | bytes 3076
  133.5 209.8 %all-gather.10.cloned.1.call-start = ((), (), s32[]{:S(2)}) async-start(), calls=%async_computation.9 | async-start | bytes 17825792 | tf_op jit(solution)/shard_map/all_gather | solution.py:723
  142.7 73.4 %copy-start.55 = (f32[2048]{0:T(1024)}, f32[2048]{0:T(1024)S(1)}, u32[]{:S(2)}) copy-start(f32[2048]{0:T(1024)S(1)} %get-tuple-element.158) | copy-start | bytes 24580
  146.2 19.8 %copy-start.13 = (f32[256,576]{1,0:T(8,128)}, f32[256,576]{1,0:T(8,128)S(1)}, u32[]{:S(2)}) copy-start(f32[256,576]{1,0:T(8,128)S(1)} %fusion.32) | copy-start | bytes 1769476
  175.3 14.7 %copy-start.57 = (f32[8,256]{1,0:T(8,128)}, f32[8,256]{1,0:T(8,128)S(1)}, u32[]{:S(2)}) copy-start(f32[8,256]{1,0:T(8,128)S(1)} %log_add_fusion) | copy-start | bytes 24580
  175.8 14.2 %copy-start.21 = (bf16[8,128,256]{2,1,0:T(8,128)(2,1)}, bf16[8,128,256]{2,1,0:T(8,128)(2,1)S(1)}, u32[]{:S(2)}) copy-start(bf16[8,128,256]{2,1,0:T(8,128)(2,1)S(1)} %convolution_convert_fusion.8) | copy-start | bytes 1572868
  186.4 28.9 %copy-start.11 = (bf16[256,2048]{1,0:T(8,128)(2,1)S(1)}, bf16[256,2048]{1,0:T(8,128)(2,1)}, u32[]{:S(2)}) copy-start(bf16[256,2048]{1,0:T(8,128)(2,1)} %param.18) | copy-start | bytes 3145732
  190.0 25.4 %collective-permute-start = (bf16[256,2048]{1,0:T(8,128)(2,1)S(1)}, bf16[256,2048]{1,0:T(8,128)(2,1)S(1)}, u32[]{:S(2)}, u32[]{:S(2)}) collective-permute-start(bf16[256,2048]{1,0:T(8,128)(2,1)S(1)} %convolution_convert_fusion.4), channel_id=1, source_target_pairs={{0,1},{1,0},{2,3},{3,2},{4,5},{5,4},{6,7},{7,6},{8,9},{9,8},{10,11... | collective-permute-start | bytes 3145736 | tf_op jit(solution)/shard_map/ppermute | solution.py:587
  218.6 231.1 %all-gather.12.cloned.1.call-start = ((), (), s32[]{:S(2)}) async-start(), calls=%async_computation.10 | async-start | bytes 4456448 | tf_op jit(solution)/shard_map/all_gather | solution.py:691
  219.1 276.5 %all-gather.14.cloned.1.call-start = ((), (), s32[]{:S(2)}) async-start(), calls=%async_computation.11 | async-start | bytes 13369344 | tf_op jit(solution)/shard_map/all_gather | solution.py:725
  343.3 444.8 %reduce-scatter.5.cloned.1.call-start = ((), (), s32[]{:S(2)}) async-start(), calls=%async_computation.12 | async-start | bytes 17825792 | tf_op jit(solution)/shard_map/reduce_scatter | solution.py:841
  351.9 16.8 %copy-start.53 = (s32[16,256]{1,0:T(8,128)}, s32[16,256]{1,0:T(8,128)S(1)}, u32[]{:S(2)}) copy-start(s32[16,256]{1,0:T(8,128)S(1)} %fusion.84) | copy-start | bytes 49156
  387.3 13.1 %copy-start.15 = (bf16[2304,2048]{1,0:T(8,128)(2,1)S(1)}, bf16[2304,2048]{1,0:T(8,128)(2,1)}, u32[]{:S(2)}) copy-start(bf16[2304,2048]{1,0:T(8,128)(2,1)} %shard_map.297) | copy-start | bytes 28311556
  400.4 9.3 copy-start.72
  420.4 9.7 copy-start.77
  527.5 28.5 %copy-start.39 = (bf16[4096,88]{1,0:T(8,128)(2,1)}, bf16[4096,88]{1,0:T(8,128)(2,1)S(1)}, u32[]{:S(2)}) copy-start(bf16[4096,88]{1,0:T(8,128)(2,1)S(1)} %get-tuple-element.174) | copy-start | bytes 2162692
  527.5 28.4 %copy-start.41 = (bf16[4096,88]{1,0:T(8,128)(2,1)}, bf16[4096,88]{1,0:T(8,128)(2,1)S(1)}, u32[]{:S(2)}) copy-start(bf16[4096,88]{1,0:T(8,128)(2,1)S(1)} %get-tuple-element.175) | copy-start | bytes 2162692
  542.1 16.1 %copy-start.75 = (bf16[2304,704]{0,1:T(8,128)(2,1)S(1)}, bf16[2304,704]{0,1:T(8,128)(2,1)}, u32[]{:S(2)}) copy-start(bf16[2304,704]{0,1:T(8,128)(2,1)} %get-tuple-element.172) | copy-start | bytes 9732100
  594.1 12.8 %copy-start.54 = (s32[16,256]{1,0:T(8,128)S(1)}, s32[16,256]{1,0:T(8,128)}, u32[]{:S(2)}) copy-start(s32[16,256]{1,0:T(8,128)} %copy-done.53) | copy-start | bytes 49156
  594.1 17.4 %copy-start.29 = (bf16[4096,88]{1,0:T(8,128)(2,1)S(1)}, bf16[4096,88]{1,0:T(8,128)(2,1)}, u32[]{:S(2)}) copy-start(bf16[4096,88]{1,0:T(8,128)(2,1)} %copy-done.28) | copy-start | bytes 2162692
  594.2 183.3 %collective-permute-start.2 = (bf16[2048,2048]{1,0:T(8,128)(2,1)}, bf16[2048,2048]{1,0:T(8,128)(2,1)}, u32[]{:S(2)}, u32[]{:S(2)}) collective-permute-start(bf16[2048,2048]{1,0:T(8,128)(2,1)} %get-tuple-element.51), channel_id=1, source_target_pairs={{0,1},{1,0},{2,3},{3,2},{4,5},{5,4},{6,7},{7,6},{8,9},{9,8},{10,11... | collective-permute-start | bytes 25165832 | tf_op jit(solution)/shard_map/ppermute | solution.py:783
  608.0 49.8 %all-to-all-start.1 = ((f32[16,1,256]{2,1,0:T(1,128)}), f32[16,1,256]{2,1,0:T(1,128)S(1)}, u32[]{:S(2)}, u32[]{:S(2)}) async-start(f32[16,1,256]{2,1,0:T(1,128)} %copy.408), calls=%async_computation.2 | async-start | bytes 32768 | tf_op jit(solution)/shard_map/all_to_all | solution.py:836
  611.5 9.4 copy-start.40
  611.5 303.2 %reduce-scatter.9.cloned.1.call-start = ((), (), s32[]{:S(2)}) async-start(), calls=%async_computation.14 | async-start | bytes 4456448 | tf_op jit(solution)/shard_map/reduce_scatter | solution.py:988
  611.6 9.3 copy-start.42
  611.6 18.7 %slice-start.3 = ((s8[9437184]{0:T(1024)(128)(4,1)}), s8[4194304]{0:T(1024)(128)(4,1)S(1)}, s32[]{:S(2)}) async-start(s8[9437184]{0:T(1024)(128)(4,1)} %bitcast.234), calls=%async_computation.19 | async-start | bytes 8388608
  611.6 18.7 %slice-start.4 = ((s8[9437184]{0:T(1024)(128)(4,1)}), s8[4194304]{0:T(1024)(128)(4,1)S(1)}, s32[]{:S(2)}) async-start(s8[9437184]{0:T(1024)(128)(4,1)} %bitcast.234), calls=%async_computation.20 | async-start | bytes 8388608
  620.9 9.4 slice-start.5
  620.9 9.4 copy-start.76
  630.4 9.1 copy-start.74
  630.4 17.8 %slice-start = ((s8[9437184]{0:T(1024)(128)(4,1)}), s8[4194304]{0:T(1024)(128)(4,1)S(1)}, s32[]{:S(2)}) async-start(s8[9437184]{0:T(1024)(128)(4,1)} %bitcast.232), calls=%async_computation.16 | async-start | bytes 8388608
  630.4 17.8 %slice-start.1 = ((s8[9437184]{0:T(1024)(128)(4,1)}), s8[4194304]{0:T(1024)(128)(4,1)S(1)}, s32[]{:S(2)}) async-start(s8[9437184]{0:T(1024)(128)(4,1)} %bitcast.232), calls=%async_computation.17 | async-start | bytes 8388608
  648.2 8.9 copy-start.34
  657.8 119.6 %collective-permute-start.1 = (f32[256,16]{0,1:T(8,128)S(1)}, f32[256,16]{0,1:T(8,128)S(1)}, u32[]{:S(2)}, u32[]{:S(2)}) collective-permute-start(f32[256,16]{0,1:T(8,128)S(1)} %bitcast.271), channel_id=1, source_target_pairs={{0,1},{1,0},{2,3},{3,2},{4,5},{5,4},{6,7},{7,6},{8,9},{9,8},{10,11... | collective-permute-start | bytes 49160 | tf_op jit(solution)/shard_map/ppermute | solution.py:587
  777.4 35.5 %copy-start.56 = (f32[2048]{0:T(1024)S(1)}, f32[2048]{0:T(1024)}, u32[]{:S(2)}) copy-start(f32[2048]{0:T(1024)} %copy-done.55) | copy-start | bytes 24580
  777.4 35.5 %copy-start.67 = (f32[256]{0:T(256)S(1)}, f32[256]{0:T(256)}, u32[]{:S(2)}) copy-start(f32[256]{0:T(256)} %copy-done.66) | copy-start | bytes 3076
  777.5 35.5 %copy-start.3 = (f32[256,2048]{1,0:T(8,128)S(1)}, f32[256,2048]{1,0:T(8,128)}, u32[]{:S(2)}) copy-start(f32[256,2048]{1,0:T(8,128)} %copy-done.2) | copy-start | bytes 6291460
  788.2 24.8 %copy-start.38 = (bf16[256,2048]{1,0:T(8,128)(2,1)S(1)}, bf16[256,2048]{1,0:T(8,128)(2,1)}, u32[]{:S(2)}) copy-start(bf16[256,2048]{1,0:T(8,128)(2,1)} %reduce-scatter.5.cloned.1.call-done) | copy-start | bytes 3145732
  788.2 24.8 %collective-permute-start.3 = (bf16[256,2048]{1,0:T(8,128)(2,1)}, bf16[256,2048]{1,0:T(8,128)(2,1)S(1)}, u32[]{:S(2)}, u32[]{:S(2)}) collective-permute-start(bf16[256,2048]{1,0:T(8,128)(2,1)} %reduce-scatter.5.cloned.1.call-done), channel_id=1, source_target_pairs={{0,1},{1,0},{2,3},{3,2},{4,5},{5,4},{6,7},{7,6},{8,9},{9,8},{10,11... | collective-permute-start | bytes 3145736 | tf_op jit(solution)/shard_map/ppermute | solution.py:587
  791.7 24.0 %copy-start.31 = (bf16[256,2048]{1,0:T(8,128)(2,1)S(1)}, bf16[256,2048]{1,0:T(8,128)(2,1)}, u32[]{:S(2)}) copy-start(bf16[256,2048]{1,0:T(8,128)(2,1)} %param.21) | copy-start | bytes 3145732
  821.1 177.7 %reduce-scatter.7.cloned.1.call-start = ((), (), s32[]{:S(2)}) async-start(), calls=%async_computation.13 | async-start | bytes 8912896 | tf_op jit(solution)/shard_map/reduce_scatter | solution.py:857
  821.8 304.1 %reduce-scatter.11.cloned.1.call-start = ((), (), s32[]{:S(2)}) async-start(), calls=%async_computation.15 | async-start | bytes 11698176 | tf_op jit(solution)/shard_map/reduce_scatter | solution.py:961
  856.2 29.8 %collective-permute-start.4 = (bf16[256,2624]{0,1:T(8,128)(2,1)}, bf16[256,2624]{0,1:T(8,128)(2,1)}, u32[]{:S(2)}, u32[]{:S(2)}) collective-permute-start(bf16[256,2624]{0,1:T(8,128)(2,1)} %copy.423), channel_id=1, source_target_pairs={{0,1},{1,0},{2,3},{3,2},{4,5},{5,4},{6,7},{7,6},{8,9},{9,8},{10,11... | collective-permute-start | bytes 4030472 | tf_op jit(solution)/shard_map/ppermute | solution.py:587
  1037.0 14.0 %collective-permute-start.5 = (bf16[128,2048]{1,0:T(8,128)(2,1)S(1)}, bf16[128,2048]{1,0:T(8,128)(2,1)}, u32[]{:S(2)}, u32[]{:S(2)}) collective-permute-start(bf16[128,2048]{1,0:T(8,128)(2,1)S(1)} %copy-done.47), channel_id=1, source_target_pairs={{0,1},{1,0},{2,3},{3,2},{4,5},{5,4},{6,7},{7,6},{8,9},{9,8},{10,11... | collective-permute-start | bytes 1572872 | tf_op jit(solution)/shard_map/ppermute | solution.py:996
  1125.9 9.7 copy-start.1
  (53 other events, 191.1 us)
Sparse Core Ops, SparseCore 0:
  17.5 115.9 all-gather.5
  135.7 50.7 all-gather.7
  218.7 124.5 all-gather.9
  345.9 48.5 all-gather.11
  396.6 98.9 all-gather.13
  594.3 175.5 reduce-scatter.4
  821.2 71.0 reduce-scatter.8
  896.3 102.3 reduce-scatter.6
  1002.8 123.0 reduce-scatter.10
